TPU v7x, 32 devices: a whole 2x2x4 slice. The times are simulated.
32 devices in a mesh: dp: 2 (over x), tp: 4 (over z), cp: 4 (over y, core).
Axes of the slice: x: 2, y: 2, z: 4, core: 2. Of those that a mesh axis runs over, the one named last changes fastest.
Arguments:
- x: bfloat16 [8192, 3584], P(('dp', 'cp')), parts along dimension 0
- doc_ids: int32 [8192], P(('dp', 'cp')), parts along dimension 0
- w_query: bfloat16 [3584, 3584], P(None, 'tp')
- w_key: bfloat16 [3584, 512], P(None, 'tp')
- w_value: bfloat16 [3584, 512], P(None, 'tp')
- w_out: bfloat16 [3584, 3584], P('tp')
Outputs:
- output: bfloat16 [8192, 3584], P(('dp', 'cp')), parts along dimension 0
There are 2 independent parts. A program takes and returns all parts, laid end to end along the dimension named above; an argument that names none is the same for every part.
All inputs are finite; a program needn't handle non-finite values.
Results may differ from a plain program's by a relative error of at most 0.00734913.
Values are sent between devices in bfloat16 or wider.
A program may use at most 1 GiB of HBM per device.

v0:
```python
import jax
import jax.numpy as jnp
from jax import lax
from jax.sharding import PartitionSpec as P

HEAD_DIM = 128


def block_update(soft_state, q_blk, k_blk, v_blk, allowed):
    run_max, run_sum, out_acc = soft_state
    scores = jnp.einsum('qhgd,khd->qhgk', q_blk, k_blk, preferred_element_type=jnp.float32) * (HEAD_DIM ** -0.5)
    scores = jnp.where(allowed[:, None, None, :], scores, -jnp.inf)
    new_max = jnp.maximum(run_max, jnp.max(scores, axis=-1))
    safe_max = jnp.where(new_max == -jnp.inf, 0.0, new_max)
    prob_vals = jnp.exp(scores - safe_max[..., None])
    rescale = jnp.exp(run_max - safe_max)
    run_sum = run_sum * rescale + jnp.sum(prob_vals, axis=-1)
    out_acc = out_acc * rescale[..., None] + jnp.einsum('qhgk,khd->qhgd', prob_vals.astype(jnp.bfloat16), v_blk, preferred_element_type=jnp.float32)
    return new_max, run_sum, out_acc


def solution(mesh):
    cp_size = mesh.shape['cp']
    shift_pairs = [(dev_idx, (dev_idx + 1) % cp_size) for dev_idx in range(cp_size)]

    def local_attention(x_loc, seg_loc, w_query, w_key, w_value, w_out):
        chunk_len = x_loc.shape[0]
        kv_heads = w_key.shape[1] // HEAD_DIM
        q_per_kv = w_query.shape[1] // w_key.shape[1]
        cp_rank = lax.axis_index('cp')
        q_loc = jnp.dot(x_loc, w_query, preferred_element_type=jnp.float32).astype(jnp.bfloat16).reshape(chunk_len, kv_heads, q_per_kv, HEAD_DIM)
        k_loc = jnp.dot(x_loc, w_key, preferred_element_type=jnp.float32).astype(jnp.bfloat16).reshape(chunk_len, kv_heads, HEAD_DIM)
        v_loc = jnp.dot(x_loc, w_value, preferred_element_type=jnp.float32).astype(jnp.bfloat16).reshape(chunk_len, kv_heads, HEAD_DIM)
        q_pos = cp_rank * chunk_len + jnp.arange(chunk_len)

        def visit_block(soft_state, k_blk, v_blk, seg_kv, src_chunk):
            k_pos = src_chunk * chunk_len + jnp.arange(chunk_len)
            active = (src_chunk <= cp_rank) & (seg_kv[chunk_len - 1] >= seg_loc[0])
            allowed = (seg_loc[:, None] == seg_kv[None, :]) & (q_pos[:, None] >= k_pos[None, :])
            return lax.cond(active, lambda same_state: block_update(same_state, q_loc, k_blk, v_blk, allowed), lambda same_state: same_state, soft_state)

        init_state = (jnp.full((chunk_len, kv_heads, q_per_kv), -jnp.inf, jnp.float32), jnp.zeros((chunk_len, kv_heads, q_per_kv), jnp.float32), jnp.zeros((chunk_len, kv_heads, q_per_kv, HEAD_DIM), jnp.float32))
        soft_state = visit_block(init_state, k_loc, v_loc, seg_loc, cp_rank)

        def shift_step(step_idx, loop_state):
            soft_state, k_blk, v_blk, seg_kv = loop_state
            k_blk = lax.ppermute(k_blk, 'cp', shift_pairs)
            v_blk = lax.ppermute(v_blk, 'cp', shift_pairs)
            seg_kv = lax.ppermute(seg_kv, 'cp', shift_pairs)
            src_chunk = (cp_rank - step_idx) % cp_size
            soft_state = visit_block(soft_state, k_blk, v_blk, seg_kv, src_chunk)
            return soft_state, k_blk, v_blk, seg_kv

        soft_state = lax.fori_loop(1, cp_size, shift_step, (soft_state, k_loc, v_loc, seg_loc))[0]
        heads_out = (soft_state[2] / soft_state[1][..., None]).astype(jnp.bfloat16).reshape(chunk_len, kv_heads * q_per_kv * HEAD_DIM)
        part_out = jnp.dot(heads_out, w_out, preferred_element_type=jnp.float32)
        return lax.psum(part_out, 'tp').astype(jnp.bfloat16)

    return jax.shard_map(local_attention, mesh=mesh, in_specs=(P(('dp', 'cp'), None), P(('dp', 'cp')), P(None, 'tp'), P(None, 'tp'), P(None, 'tp'), P('tp', None)), out_specs=P(('dp', 'cp'), None), check_vma=False)
```

profile of v0, /device:TPU:6, one launch (start us, length us, event | category | flops | bytes accessed | tf_op | source)
XLA Modules:
  0.0 686.7 jit_solution(4387675940558392001)
XLA Ops:
  0.0 1.4 fusion.41
  2.6 0.0 copy-start.6
  2.6 5.3 fusion.39
  7.9 0.0 copy-start.7
  7.9 11.0 %convolution_convert_fusion = bf16[1024,896]{0,1:T(8,128)(2,1)} fusion(bf16[1024,3584]{1,0:T(8,128)(2,1)S(1)} %copy-done.6, bf16[3584,896]{1,0:T(8,128)(2,1)} %param.14), kind=kOutput, calls=%fused_computation.52 | convolution fusion | flops 6577586176 | bytes 15597568 | tf_op jit(solution)/shard_map/dot_general | solution.py:31
  18.9 2.1 fusion.40
  21.0 41.3 %conditional.2 = (f32[1024,1,7]{0,2,1:T(8,128)S(1)}, f32[1024,1,7]{0,2,1:T(8,128)S(1)}, f32[1024,1,7,128]{3,0,2,1:T(8,128)S(1)}) conditional(s32[]{:T(128)} %bitcast.31, () %tuple.47, (s32[1024]{0:T(1024)S(1)}, s32[]{:T(128)}, s32[1024,1]{0,1:T(1,128)S(1)}, s32[1,1024]{1,0:T(1,128)S(1)}, bf16[1024,1,128]{2,0,1:T(8,128)(2,1)S(1)}, ...), branch_computations={%region_0.0_spmd, %region_1.4_spmd} | conditional | flops 3842952192 | bytes 98877528 | solution.py:40
  21.2 1.2 compare_and_fusion
  22.4 13.6 %fusion.4 = (f32[1024,7]{0,1:T(8,128)S(1)}, f32[1024,1024,7]{1,0,2:T(8,128)}) fusion(pred[1024,1024]{0,1:T(8,128)(4,1)S(1)} %compare_and_fusion, bf16[1024,1,7,128]{0,3,2,1:T(8,128)(2,1)} %get-tuple-element.457, bf16[1024,1,128]{2,0,1:T(8,128)(2,1)S(1)} %get-tuple-element.367), kind=kOutput, calls=%fused_computation.5 | convolution fusion | flops 1901061120 | bytes 32534528 | tf_op jit(solution)/shard_map/cond/branch_1_fun/qhgd,khd->qhgk/dot_general | solution.py:11
  36.1 13.4 %fusion.3 = f32[1024,7]{0,1:T(8,128)S(1)} fusion(f32[1024,1024,7]{1,0,2:T(8,128)} %get-tuple-element.500, f32[1024,7]{0,1:T(8,128)S(1)} %get-tuple-element.498, pred[1024,1024]{0,1:T(8,128)(4,1)S(1)} %compare_and_fusion), kind=kLoop, calls=%fused_computation.4 | loop fusion | flops 29352960 | bytes 30466048 | tf_op jit(solution)/shard_map/cond/branch_1_fun/reduce_sum | solution.py:17
  49.5 0.0 copy-start.4
  49.5 12.5 %fusion.9 = f32[1024,1,7,128]{3,0,2,1:T(8,128)S(1)} fusion(f32[1024,1024,7]{1,0,2:T(8,128)} %get-tuple-element.500, f32[1024,7]{0,1:T(8,128)S(1)} %get-tuple-element.498, pred[1024,1024]{0,1:T(8,128)(4,1)S(1)} %compare_and_fusion, f32[1024,7]{0,1:T(8,128)S(1)} %get-tuple-element.497, bf16[1024,1,128]{2,0,1:T(8,128)(2,1)S(1)} %get-tuple-element.369), kind=kOutput, calls=%fused_computation.11 | convolution fusion | flops 1909325824 | bytes 34398208 | tf_op jit(solution)/shard_map/cond/branch_1_fun/qhgk,khd->qhgd/dot_general | solution.py:18
  62.3 0.0 copy-start.2
  62.3 1.8 copy-done.2
  64.1 3.0 copy.14
  67.1 115.9 %while.26 = (s32[]{:T(128)}, f32[1024,1,7]{0,2,1:T(8,128)S(1)}, f32[1024,1,7]{0,2,1:T(8,128)S(1)}, f32[1024,1,7,128]{3,0,2,1:T(8,128)}, bf16[1024,1,128]{2,0,1:T...) while((s32[]{:T(128)}, f32[1024,1,7]{0,2,1:T(8,128)S(1)}, ...), condition=%wide.region_9.10_spmd.clone, body=%wide.region_4.9_spmd.clone.sunk | while | flops 3843884032 | bytes 105701968 | solution.py:54
  67.1 0.1 collective-permute-start.1
  67.2 0.6 collective-permute-start.2
  67.8 0.1 collective-permute-start
  67.9 0.5 slice.35
  68.3 7.5 %collective-permute-done = s32[1024]{0:T(1024)S(1)} collective-permute-done((s32[1024]{0:T(1024)S(1)}, s32[1024]{0:T(1024)S(1)}, u32[]{:S(2)}, u32[]{:S(2)}) %collective-permute-start) | collective-permute-done | bytes 4128 | tf_op jit(solution)/shard_map/while/body/eval_jaxpr/ppermute | solution.py:49
  75.8 0.6 slice.34
  77.7 42.1 %conditional.5 = ((f32[1024,1,7]{0,2,1:T(8,128)S(1)}, f32[1024,1,7]{0,2,1:T(8,128)S(1)}, f32[1024,1,7,128]{3,0,2,1:T(8,128)})) conditional(s32[]{:T(128)} %convert_element_type.68, (f32[1024,1,7]{0,2,1:T(8,128)S(1)}, f32[1024,1,7]{0,2,1:T(8,128)S(1)}, f32[1024,1,7,128]{3,0,2,1:T(8,128)}) %tuple.74, (s32[1024]{0:T(1024)S(1)}, s32[1024]{0:T(1024)S(1)}, ...), branch_computations={%region_5.5_spmd, %region_6.8_spmd} | conditional | flops 3843884032 | bytes 102522928 | solution.py:40
  77.7 1.2 compare_and_fusion.1
  78.9 11.9 %fusion.24 = (f32[1024,7]{0,1:T(8,128)S(1)}, f32[1024,1024,7]{1,0,2:T(8,128)}) fusion(pred[1024,1024]{0,1:T(8,128)(4,1)S(1)} %compare_and_fusion.1, bf16[1024,1,7,128]{3,0,2,1:T(8,128)(2,1)S(1)} %get-tuple-element.377, bf16[1024,1,128]{2,0,1:T(8,128)(2,1)S(1)} %get-tuple-element.376), kind=kOutput, calls=%fused_computation.31 | convolution fusion | flops 1901061120 | bytes 32534528 | tf_op jit(solution)/shard_map/while/body/eval_jaxpr/cond/branch_1_fun/qhgd,khd->qhgk/dot_general | solution.py:11
  90.9 13.4 %fusion.23 = f32[1024,7]{0,1:T(8,128)S(1)} fusion(f32[1024,1024,7]{1,0,2:T(8,128)} %get-tuple-element.502, f32[1024,7]{0,1:T(8,128)S(1)} %fusion.35, pred[1024,1024]{0,1:T(8,128)(4,1)S(1)} %compare_and_fusion.1), kind=kLoop, calls=%fused_computation.30 | loop fusion | flops 29352960 | bytes 30466048 | tf_op jit(solution)/shard_map/while/body/eval_jaxpr/cond/branch_1_fun/reduce_sum | solution.py:17
  104.3 15.4 %bitcast_add_fusion.1 = f32[1024,1,7,128]{3,0,2,1:T(8,128)} fusion(f32[1024,1,7,128]{3,0,2,1:T(8,128)} %get-tuple-element.379, f32[1024,1024,7]{1,0,2:T(8,128)} %get-tuple-element.502, f32[1024,7]{0,1:T(8,128)S(1)} %fusion.35, pred[1024,1024]{0,1:T(8,128)(4,1)S(1)} %compare_and_fusion.1, f32[1024,7]{0,1:T(8,128)S(1)} %get-tuple-element.495, ...), kind=kOutput, calls=%fused_computation.36 | convolution fusion | flops 1910243328 | bytes 38068224 | tf_op jit(solution)/shard_map/while/body/eval_jaxpr/cond/branch_1_fun/qhgk,khd->qhgd/dot_general | solution.py:18
  119.8 0.1 collective-permute-start.1
  119.9 0.1 collective-permute-start.2
  119.9 0.1 collective-permute-start
  120.0 0.5 slice.35
  120.5 8.0 %collective-permute-done = s32[1024]{0:T(1024)S(1)} collective-permute-done((s32[1024]{0:T(1024)S(1)}, s32[1024]{0:T(1024)S(1)}, u32[]{:S(2)}, u32[]{:S(2)}) %collective-permute-start) | collective-permute-done | bytes 4128 | tf_op jit(solution)/shard_map/while/body/eval_jaxpr/ppermute | solution.py:49
  128.5 0.6 slice.34
  130.3 42.1 %conditional.5 = ((f32[1024,1,7]{0,2,1:T(8,128)S(1)}, f32[1024,1,7]{0,2,1:T(8,128)S(1)}, f32[1024,1,7,128]{3,0,2,1:T(8,128)})) conditional(s32[]{:T(128)} %convert_element_type.68, (f32[1024,1,7]{0,2,1:T(8,128)S(1)}, f32[1024,1,7]{0,2,1:T(8,128)S(1)}, f32[1024,1,7,128]{3,0,2,1:T(8,128)}) %tuple.74, (s32[1024]{0:T(1024)S(1)}, s32[1024]{0:T(1024)S(1)}, ...), branch_computations={%region_5.5_spmd, %region_6.8_spmd} | conditional | flops 3843884032 | bytes 102522928 | solution.py:40
  130.4 1.2 compare_and_fusion.1
  131.6 11.9 %fusion.24 = (f32[1024,7]{0,1:T(8,128)S(1)}, f32[1024,1024,7]{1,0,2:T(8,128)}) fusion(pred[1024,1024]{0,1:T(8,128)(4,1)S(1)} %compare_and_fusion.1, bf16[1024,1,7,128]{3,0,2,1:T(8,128)(2,1)S(1)} %get-tuple-element.377, bf16[1024,1,128]{2,0,1:T(8,128)(2,1)S(1)} %get-tuple-element.376), kind=kOutput, calls=%fused_computation.31 | convolution fusion | flops 1901061120 | bytes 32534528 | tf_op jit(solution)/shard_map/while/body/eval_jaxpr/cond/branch_1_fun/qhgd,khd->qhgk/dot_general | solution.py:11
  143.5 13.4 %fusion.23 = f32[1024,7]{0,1:T(8,128)S(1)} fusion(f32[1024,1024,7]{1,0,2:T(8,128)} %get-tuple-element.502, f32[1024,7]{0,1:T(8,128)S(1)} %fusion.35, pred[1024,1024]{0,1:T(8,128)(4,1)S(1)} %compare_and_fusion.1), kind=kLoop, calls=%fused_computation.30 | loop fusion | flops 29352960 | bytes 30466048 | tf_op jit(solution)/shard_map/while/body/eval_jaxpr/cond/branch_1_fun/reduce_sum | solution.py:17
  157.0 15.4 %bitcast_add_fusion.1 = f32[1024,1,7,128]{3,0,2,1:T(8,128)} fusion(f32[1024,1,7,128]{3,0,2,1:T(8,128)} %get-tuple-element.379, f32[1024,1024,7]{1,0,2:T(8,128)} %get-tuple-element.502, f32[1024,7]{0,1:T(8,128)S(1)} %fusion.35, pred[1024,1024]{0,1:T(8,128)(4,1)S(1)} %compare_and_fusion.1, f32[1024,7]{0,1:T(8,128)S(1)} %get-tuple-element.495, ...), kind=kOutput, calls=%fused_computation.36 | convolution fusion | flops 1910243328 | bytes 38068224 | tf_op jit(solution)/shard_map/while/body/eval_jaxpr/cond/branch_1_fun/qhgk,khd->qhgd/dot_general | solution.py:18
  172.4 0.1 collective-permute-start.1
  172.5 0.1 collective-permute-start.2
  172.6 0.1 collective-permute-start
  172.7 0.5 slice.35
  173.1 8.0 %collective-permute-done = s32[1024]{0:T(1024)S(1)} collective-permute-done((s32[1024]{0:T(1024)S(1)}, s32[1024]{0:T(1024)S(1)}, u32[]{:S(2)}, u32[]{:S(2)}) %collective-permute-start) | collective-permute-done | bytes 4128 | tf_op jit(solution)/shard_map/while/body/eval_jaxpr/ppermute | solution.py:49
  181.1 0.6 slice.34
  183.0 5.1 copy.15
  188.1 2.6 divide_convert_fusion
  190.7 14.2 %fusion.42 = f32[1024,3584]{1,0:T(8,128)} fusion(bf16[1024,896]{0,1:T(8,128)(2,1)S(1)} %bitcast.121, bf16[896,3584]{1,0:T(8,128)(2,1)} %param.17), kind=kOutput, calls=%fused_computation.58 | convolution fusion | flops 6576668672 | bytes 22937600 | tf_op jit(solution)/shard_map/dot_general | solution.py:56
  204.9 481.8 %all-reduce.1 = bf16[1024,3584]{1,0:T(8,128)(2,1)} all-reduce(f32[1024,3584]{1,0:T(8,128)} %fusion.42), channel_id=1, replica_groups=mesh['dp'=2,'tp'=4,'cp'=4] {'tp'}, use_global_device_ids=true, to_apply=%region_10.11 | all-reduce | flops 3670016 | bytes 22020096 | tf_op jit(solution)/shard_map/psum | solution.py:57
  (52 shorter events, 0.4 us)
Async XLA Ops:
  0.0 2.6 copy-start
  2.6 5.3 copy-start.6
  7.9 11.0 %copy-start.7 = (bf16[3584,128]{1,0:T(8,128)(2,1)S(1)}, bf16[3584,128]{1,0:T(8,128)(2,1)}, u32[]{:S(2)}) copy-start(bf16[3584,128]{1,0:T(8,128)(2,1)} %param.16) | copy-start | bytes 2752516
  18.9 2.1 copy-start.5
  36.0 13.4 %copy-start.3 = (f32[1024,7]{0,1:T(8,128)}, f32[1024,7]{0,1:T(8,128)S(1)}, u32[]{:S(2)}) copy-start(f32[1024,7]{0,1:T(8,128)S(1)} %get-tuple-element.499) | copy-start | bytes 86020 | tf_op jit(solution)/shard_map/cond
  49.5 12.6 %copy-start.4 = (f32[1024,7]{0,1:T(8,128)S(1)}, f32[1024,7]{0,1:T(8,128)}, u32[]{:S(2)}) copy-start(f32[1024,7]{0,1:T(8,128)} %copy-done.3) | copy-start | bytes 86020 | tf_op jit(solution)/shard_map/cond
  62.3 1.8 copy-start.2
  67.1 10.5 %collective-permute-start.1 = (bf16[1024,1,128]{2,0,1:T(8,128)(2,1)S(1)}, bf16[1024,1,128]{2,0,1:T(8,128)(2,1)S(1)}, u32[]{:S(2)}, u32[]{:S(2)}) collective-permute-start(bf16[1024,1,128]{2,0,1:T(8,128)(2,1)S(1)} %get-tuple-element.609), channel_id=1, source_target_pairs={{0,1},{1,2},{2,3},{3,0},{4,5},{5,6},{6,7},{7,4},{8,9},{9,10},{10,1... | collective-permute-start | bytes 786440 | tf_op jit(solution)/shard_map/while/body/eval_jaxpr/ppermute | solution.py:47
  67.2 10.4 %collective-permute-start.2 = (bf16[1024,1,128]{2,0,1:T(8,128)(2,1)S(1)}, bf16[1024,1,128]{2,0,1:T(8,128)(2,1)S(1)}, u32[]{:S(2)}, u32[]{:S(2)}) collective-permute-start(bf16[1024,1,128]{2,0,1:T(8,128)(2,1)S(1)} %get-tuple-element.610), channel_id=1, source_target_pairs={{0,1},{1,2},{2,3},{3,0},{4,5},{5,6},{6,7},{7,4},{8,9},{9,10},{10,1... | collective-permute-start | bytes 786440 | tf_op jit(solution)/shard_map/while/body/eval_jaxpr/ppermute | solution.py:48
  67.8 8.0 %collective-permute-start = (s32[1024]{0:T(1024)S(1)}, s32[1024]{0:T(1024)S(1)}, u32[]{:S(2)}, u32[]{:S(2)}) collective-permute-start(s32[1024]{0:T(1024)S(1)} %get-tuple-element.611), channel_id=1, source_target_pairs={{0,1},{1,2},{2,3},{3,0},{4,5},{5,6},{6,7},{7,4},{8,9},{9,10},{10,1... | collective-permute-start | bytes 12296 | tf_op jit(solution)/shard_map/while/body/eval_jaxpr/ppermute | solution.py:49
  119.8 10.5 %collective-permute-start.1 = (bf16[1024,1,128]{2,0,1:T(8,128)(2,1)S(1)}, bf16[1024,1,128]{2,0,1:T(8,128)(2,1)S(1)}, u32[]{:S(2)}, u32[]{:S(2)}) collective-permute-start(bf16[1024,1,128]{2,0,1:T(8,128)(2,1)S(1)} %get-tuple-element.609), channel_id=1, source_target_pairs={{0,1},{1,2},{2,3},{3,0},{4,5},{5,6},{6,7},{7,4},{8,9},{9,10},{10,1... | collective-permute-start | bytes 786440 | tf_op jit(solution)/shard_map/while/body/eval_jaxpr/ppermute | solution.py:47
  119.9 10.4 %collective-permute-start.2 = (bf16[1024,1,128]{2,0,1:T(8,128)(2,1)S(1)}, bf16[1024,1,128]{2,0,1:T(8,128)(2,1)S(1)}, u32[]{:S(2)}, u32[]{:S(2)}) collective-permute-start(bf16[1024,1,128]{2,0,1:T(8,128)(2,1)S(1)} %get-tuple-element.610), channel_id=1, source_target_pairs={{0,1},{1,2},{2,3},{3,0},{4,5},{5,6},{6,7},{7,4},{8,9},{9,10},{10,1... | collective-permute-start | bytes 786440 | tf_op jit(solution)/shard_map/while/body/eval_jaxpr/ppermute | solution.py:48
  119.9 8.6 %collective-permute-start = (s32[1024]{0:T(1024)S(1)}, s32[1024]{0:T(1024)S(1)}, u32[]{:S(2)}, u32[]{:S(2)}) collective-permute-start(s32[1024]{0:T(1024)S(1)} %get-tuple-element.611), channel_id=1, source_target_pairs={{0,1},{1,2},{2,3},{3,0},{4,5},{5,6},{6,7},{7,4},{8,9},{9,10},{10,1... | collective-permute-start | bytes 12296 | tf_op jit(solution)/shard_map/while/body/eval_jaxpr/ppermute | solution.py:49
  172.4 10.5 %collective-permute-start.1 = (bf16[1024,1,128]{2,0,1:T(8,128)(2,1)S(1)}, bf16[1024,1,128]{2,0,1:T(8,128)(2,1)S(1)}, u32[]{:S(2)}, u32[]{:S(2)}) collective-permute-start(bf16[1024,1,128]{2,0,1:T(8,128)(2,1)S(1)} %get-tuple-element.609), channel_id=1, source_target_pairs={{0,1},{1,2},{2,3},{3,0},{4,5},{5,6},{6,7},{7,4},{8,9},{9,10},{10,1... | collective-permute-start | bytes 786440 | tf_op jit(solution)/shard_map/while/body/eval_jaxpr/ppermute | solution.py:47
  172.5 10.4 %collective-permute-start.2 = (bf16[1024,1,128]{2,0,1:T(8,128)(2,1)S(1)}, bf16[1024,1,128]{2,0,1:T(8,128)(2,1)S(1)}, u32[]{:S(2)}, u32[]{:S(2)}) collective-permute-start(bf16[1024,1,128]{2,0,1:T(8,128)(2,1)S(1)} %get-tuple-element.610), channel_id=1, source_target_pairs={{0,1},{1,2},{2,3},{3,0},{4,5},{5,6},{6,7},{7,4},{8,9},{9,10},{10,1... | collective-permute-start | bytes 786440 | tf_op jit(solution)/shard_map/while/body/eval_jaxpr/ppermute | solution.py:48
  172.6 8.6 %collective-permute-start = (s32[1024]{0:T(1024)S(1)}, s32[1024]{0:T(1024)S(1)}, u32[]{:S(2)}, u32[]{:S(2)}) collective-permute-start(s32[1024]{0:T(1024)S(1)} %get-tuple-element.611), channel_id=1, source_target_pairs={{0,1},{1,2},{2,3},{3,0},{4,5},{5,6},{6,7},{7,4},{8,9},{9,10},{10,1... | collective-permute-start | bytes 12296 | tf_op jit(solution)/shard_map/while/body/eval_jaxpr/ppermute | solution.py:49
  190.7 496.0 %copy-start.1 = (bf16[3584,128]{1,0:T(8,128)(2,1)S(1)}, bf16[3584,128]{1,0:T(8,128)(2,1)}, u32[]{:S(2)}) copy-start(bf16[3584,128]{1,0:T(8,128)(2,1)} %param.15) | copy-start | bytes 2752516
where the time goes:
time: 692 us; the launch traced here: 687 us
  blocking collectives  482 us (70%)
  matrix products  113 us (16%)
  other arithmetic  46.5 us (7%)
  waiting for transfers between devices  23.5 us (3%)
  local copies, waits for them, and re-layouts  14.6 us (2%)
    psum x1, blocking collectives, local_attention(): return lax.psum(part_out, 'tp').astype(jnp.bfloat16)  482 us
    dot_general x3, matrix products, block_update(): jnp.einsum('qhgk,khd->qhgd', prob_vals.astype(jnp.bfloat16), v_blk, prefe...  43.3 us
    reduce_sum x3, other arithmetic, block_update(): run_sum = run_sum * rescale + jnp.sum(prob_vals, axis=-1)  40.2 us
    dot_general x3, matrix products, block_update(): jnp.einsum('qhgd,khd->qhgk', q_blk, k_blk, preferred_element_type=jnp.flo...  37.5 us
    ppermute x3, waiting for transfers between devices, shift_step(): seg_kv = lax.ppermute(seg_kv, 'cp', shift_pairs)  23.5 us
    dot_general x1, matrix products, local_attention(): part_out = jnp.dot(heads_out, w_out, preferred_element_type=jnp.float32)  14.2 us
  transfers between devices with their start and end apart: 9, of which 3 were waited for; matrix products, arithmetic and copies ran while one was open for 0% of the time, Pallas kernels for 0%

commit v1 on v0

v1 whole, which is shorter than its diff:
```python
import functools

import jax
import jax.numpy as jnp
from jax import lax
from jax.experimental import pallas as pl
from jax.experimental.pallas import tpu as pltpu
from jax.sharding import PartitionSpec as P

HEAD_DIM = 128
MESH = pl.DeviceIdType.MESH
LOG2_SCALE = (HEAD_DIM ** -0.5) * 1.4426950408889634
F32 = jnp.float32
BF16 = jnp.bfloat16

Q_BLK = 256
LOC_BLK = 512
O_ROWS = 128


def coords():
    return lax.axis_index('dp'), lax.axis_index('tp'), lax.axis_index('cp')


def greet(dp, tp, cp, mid):
    bar = pltpu.get_barrier_semaphore()

    def hello(dev):
        pl.semaphore_signal(bar, inc=1, device_id=dev, device_id_type=MESH)

    hello((1 - dp, tp, cp))
    hello((dp, tp, lax.rem(cp + 2, 4)))
    hello((dp, tp, cp + 1 - 2 * lax.rem(cp, 2)))
    pl.when(tp > 0)(lambda: hello((dp, tp - 1, cp)))
    pl.when(tp < 3)(lambda: hello((dp, tp + 1, cp)))
    pl.semaphore_wait(bar, 4 + mid)


def peer_shard(tp, k):
    if k == 1:
        return tp + 1 - 2 * lax.rem(tp, 2)
    if k == 2:
        return lax.rem(tp + 2, 4)
    return 3 - tp


def attend_kernel(x_hbm, seg_col, seg_row, wq_hbm, wk_hbm, wv_hbm, wo_hbm, o_ref, wz_hbm,
                  x_v, wq_v, wkv_v, q_v, kv_v, seg_v, bias_v, m_v, l_v, acc_v,
                  load_sem, kv_send, kv_recv, seg_send, seg_recv, z_send, z_recv):
    dp, tp, cp = coords()
    mid = lax.rem((tp + 1) // 2, 2)
    core = lax.rem(cp, 2)
    chunk = x_v.shape[0]
    heads = q_v.shape[1] // HEAD_DIM
    n_rows = wo_hbm.shape[0] // 8
    n_blk = chunk // Q_BLK

    loads = []
    for i in range(n_blk):
        rows = slice(i * Q_BLK, (i + 1) * Q_BLK)
        loads.append(pltpu.make_async_copy(x_hbm.at[rows], x_v.at[rows], load_sem.at[i]))
    k_load = pltpu.make_async_copy(wk_hbm, wkv_v.at[:, 0:HEAD_DIM], load_sem.at[n_blk])
    v_load = pltpu.make_async_copy(wv_hbm, wkv_v.at[:, HEAD_DIM:2 * HEAD_DIM], load_sem.at[n_blk + 1])
    q_load = pltpu.make_async_copy(wq_hbm, wq_v, load_sem.at[n_blk + 2])
    k_load.start()
    v_load.start()
    for load in loads:
        load.start()
    q_load.start()

    greet(dp, tp, cp, mid)

    mine = pl.ds(pl.multiple_of((dp * 4 + cp) * n_rows, 16), n_rows)

    def z_copy(slot, src, shard, to):
        return pltpu.make_async_remote_copy(src, wz_hbm.at[shard], z_send.at[slot], z_recv.at[shard],
                                            device_id=(dp, to, cp), device_id_type=MESH)

    z_up = z_copy(0, wo_hbm.at[mine], tp, tp + 1)
    z_down = z_copy(4, wo_hbm.at[mine], tp, tp - 1)
    pl.when(tp < 3)(z_up.start)
    pl.when(tp > 0)(z_down.start)

    def z_next(k):
        shard = peer_shard(tp, k)
        to = tp + 1 - 2 * (shard // (tp + 1) > 0).astype(jnp.int32)
        return z_copy(k, wz_hbm.at[shard], shard, to)

    def z_forward(k):
        z_next(k).wait_recv()

        @pl.when(mid == 1)
        def _():
            z_next(k).start()

    own = pl.ds(pl.multiple_of(cp * chunk, chunk), chunk)
    k_load.wait()
    v_load.wait()
    for i in range(n_blk):
        loads[i].wait()
        rows = slice(i * Q_BLK, (i + 1) * Q_BLK)
        kv_v[pl.ds(pl.multiple_of(cp * chunk + i * Q_BLK, Q_BLK), Q_BLK), :] = jnp.dot(
            x_v[rows, :], wkv_v[...], preferred_element_type=F32).astype(BF16)
    seg_load = pltpu.make_async_copy(seg_row, seg_v.at[:, own], load_sem.at[n_blk + 3])
    seg_load.start()
    seg_load.wait()

    def kv_copies(slot, block, to):
        rows = pl.ds(pl.multiple_of(block * chunk, chunk), chunk)
        dev = (dp, tp, to)
        return (pltpu.make_async_remote_copy(kv_v.at[rows], kv_v.at[rows], kv_send.at[slot], kv_recv.at[slot],
                                             device_id=dev, device_id_type=MESH),
                pltpu.make_async_remote_copy(seg_v.at[:, rows], seg_v.at[:, rows], seg_send.at[slot], seg_recv.at[slot],
                                             device_id=dev, device_id_type=MESH))

    def over(copies, what):
        for copy in copies:
            getattr(copy, what)()

    other_core = cp + 1 - 2 * core

    q_load.wait()

    def project(i):
        rows = pl.ds(pl.multiple_of(i * Q_BLK, Q_BLK), Q_BLK)
        q_v[rows, :] = jnp.dot(x_v[rows, :], wq_v[...], preferred_element_type=F32).astype(BF16)

    project(0)
    pl.when(cp < 2)(lambda: over(kv_copies(0, cp, lax.rem(cp + 2, 4)), 'start'))
    pl.when(core == 0)(lambda: over(kv_copies(1, cp, other_core), 'start'))

    @pl.loop(1, n_blk)
    def _(i):
        project(i)

    def step(i, key0, n_keys, first, local):
        rows = pl.ds(pl.multiple_of(i * Q_BLK, Q_BLK), Q_BLK)
        keys = pl.ds(pl.multiple_of(key0, n_keys), n_keys)
        groups = n_keys // HEAD_DIM
        q_seg = seg_col[rows, :]
        for g in range(groups):
            cols = pl.ds(pl.multiple_of(key0 + g * HEAD_DIM, HEAD_DIM), HEAD_DIM)
            ok = q_seg == seg_v[0:1, cols]
            if local:
                q_pos = cp * chunk + i * Q_BLK + lax.broadcasted_iota(jnp.int32, (Q_BLK, HEAD_DIM), 0)
                k_pos = key0 + g * HEAD_DIM + lax.broadcasted_iota(jnp.int32, (Q_BLK, HEAD_DIM), 1)
                ok = ok & (q_pos >= k_pos)
            bias_v[:, g * HEAD_DIM:(g + 1) * HEAD_DIM] = jnp.where(ok, 0.0, -jnp.inf)
        k_blk = kv_v[keys, 0:HEAD_DIM]
        v_blk = kv_v[keys, HEAD_DIM:2 * HEAD_DIM]
        for h in range(heads):
            cols = slice(h * HEAD_DIM, (h + 1) * HEAD_DIM)
            s = lax.dot_general(q_v[rows, cols], k_blk, (((1,), (1,)), ((), ())), preferred_element_type=F32)
            s = [s[:, g * HEAD_DIM:(g + 1) * HEAD_DIM] + bias_v[:, g * HEAD_DIM:(g + 1) * HEAD_DIM] for g in range(groups)]
            top = functools.reduce(jnp.maximum, s)
            top = jnp.max(top, axis=1, keepdims=True)
            if first:
                m_new = jnp.broadcast_to(top, (Q_BLK, HEAD_DIM))
            else:
                m_old = m_v[rows, cols]
                m_new = jnp.maximum(m_old, top)
                fade = jnp.exp2((m_old - m_new) * LOG2_SCALE)
            p = [jnp.exp2((part - m_new) * LOG2_SCALE) for part in s]
            total = functools.reduce(jnp.add, p)
            probs = jnp.concatenate([part.astype(BF16) for part in p], axis=1)
            pv = jnp.dot(probs, v_blk, preferred_element_type=F32)
            m_v[rows, cols] = m_new
            if first:
                l_v[rows, cols] = total
                acc_v[rows, cols] = pv
            else:
                l_v[rows, cols] = l_v[rows, cols] * fade + total
                acc_v[rows, cols] = acc_v[rows, cols] * fade + pv

    per_loc = LOC_BLK // Q_BLK

    def local_pass(i):
        last = i // per_loc
        step(i, cp * chunk + last * LOC_BLK, LOC_BLK, True, True)

        @pl.loop(0, last)
        def _(j):
            step(i, cp * chunk + j * LOC_BLK, LOC_BLK, False, False)

    @pl.loop(0, n_blk)
    def _(i):
        local_pass(i)

    z_forward(1)
    z_forward(3)

    @pl.when(cp >= 2)
    def _():
        over(kv_copies(0, cp - 2, cp), 'wait_recv')
        over(kv_copies(2, cp - 2, other_core), 'start')
        over(kv_copies(2, other_core - 2, cp), 'wait_recv')

    @pl.when(core == 1)
    def _():
        over(kv_copies(1, other_core, cp), 'wait_recv')

    def finish(i):
        rows = pl.ds(pl.multiple_of(i * Q_BLK, Q_BLK), Q_BLK)
        for h in range(heads):
            cols = slice(h * HEAD_DIM, (h + 1) * HEAD_DIM)
            total = jnp.sum(l_v[rows, cols], axis=1, keepdims=True)
            o_ref[rows, cols] = (acc_v[rows, cols] / total).astype(BF16)

    @pl.loop(0, n_blk)
    def _(i):
        @pl.loop(0, cp)
        def _(j):
            step(i, j * chunk, chunk, False, False)

        finish(i)

        @pl.when(i == 1)
        def _():
            z_forward(2)

    pl.when(cp < 2)(lambda: over(kv_copies(0, cp, lax.rem(cp + 2, 4)), 'wait_send'))
    pl.when(core == 0)(lambda: over(kv_copies(1, cp, other_core), 'wait_send'))
    pl.when(cp >= 2)(lambda: over(kv_copies(2, cp - 2, other_core), 'wait_send'))
    pl.when(tp < 3)(z_up.wait_send)
    pl.when(tp > 0)(z_down.wait_send)

    @pl.when(mid == 1)
    def _():
        for k in (1, 2, 3):
            z_next(k).wait_send()


def output_kernel(o_hbm, wo_hbm, wz_hbm, y_hbm, w_v, o_v, acc_v, y_v,
                  load_sem, own_sem, w_send, w_recv, o_send, o_recv, y_sem):
    dp, tp, cp = coords()
    mid = lax.rem((tp + 1) // 2, 2)
    chunk, width = o_hbm.shape
    n_cols = wo_hbm.shape[1]
    n_rows = width // 8
    half = n_cols // 2
    n_pc = chunk // O_ROWS
    cp_y = lax.rem(cp + 2, 4)
    cp_c = cp + 1 - 2 * lax.rem(cp, 2)
    dev_x, dev_y, dev_c = (1 - dp, tp, cp), (dp, tp, cp_y), (dp, tp, cp_c)

    own_w = pltpu.make_async_copy(wo_hbm, w_v.at[0], load_sem.at[0])
    own_o = pltpu.make_async_copy(o_hbm, o_v.at[tp], load_sem.at[1])
    own_w.start()
    own_o.start()

    greet(dp, tp, cp, mid)

    def piece(c):
        return pl.ds(pl.multiple_of(c * O_ROWS, O_ROWS), O_ROWS)

    def o_copy(slot, c, src, shard, to):
        return pltpu.make_async_remote_copy(src, o_v.at[shard, piece(c)], o_send.at[slot, c], o_recv.at[shard, c],
                                            device_id=(dp, to, cp), device_id_type=MESH)

    def o_up(c):
        return o_copy(0, c, o_hbm.at[piece(c)], tp, tp + 1)

    def o_down(c):
        return o_copy(4, c, o_hbm.at[piece(c)], tp, tp - 1)

    @pl.loop(0, n_pc)
    def _(c):
        pl.when(tp < 3)(lambda: o_up(c).start())
        pl.when(tp > 0)(lambda: o_down(c).start())

    def o_next(k, c):
        shard = peer_shard(tp, k)
        to = tp + 1 - 2 * (shard // (tp + 1) > 0).astype(jnp.int32)
        return o_copy(k, c, o_v.at[shard, piece(c)], shard, to)

    def o_forward(k, c):
        o_next(k, c).wait_recv()
        pl.when(mid == 1)(lambda: o_next(k, c).start())

    def rows_of(dp_i, cp_i):
        return pl.ds(pl.multiple_of((dp_i * 4 + cp_i) * n_rows, 16), n_rows)

    cols = {'a': pl.ds(0, half), 'b': pl.ds(half, half), 'ab': pl.ds(0, n_cols)}
    hops = [('x', 'own', 'a'), ('x', 'own', 'b'), ('x', 'y', 'b'), ('y', 'own', 'b'), ('y', 'own', 'a'), ('y', 'x', 'a'),
            ('c', 'own', 'ab'), ('c', 'x', 'a'), ('c', 'x', 'b'), ('c', 'd', 'b'), ('c', 'y', 'b'), ('c', 'y', 'a'), ('c', 'd', 'a')]

    def slice_rows(name, dp_i, cp_i):
        far = lax.rem(cp_i + 2, 4)
        return {'own': rows_of(dp_i, cp_i), 'x': rows_of(1 - dp_i, cp_i), 'y': rows_of(dp_i, far), 'd': rows_of(1 - dp_i, far)}[name]

    def w_copy(k, hop):
        route, name, part = hops[hop]
        rows, cut = slice_rows(name, dp, cp), cols[part]
        dst = w_v.at[k, rows, cut]
        src = wz_hbm.at[peer_shard(tp, k), :, cut] if name == 'own' else dst
        dev = {'x': dev_x, 'y': dev_y, 'c': dev_c}[route]
        return pltpu.make_async_remote_copy(src, dst, w_send.at[k - 1, hop], w_recv.at[k - 1, hop], device_id=dev, device_id_type=MESH)

    def w_arrival(k, hop):
        route, name, part = hops[hop]
        dp_i, cp_i = {'x': (1 - dp, cp), 'y': (dp, cp_y), 'c': (dp, cp_c)}[route]
        dst = w_v.at[k, slice_rows(name, dp_i, cp_i), cols[part]]
        dev = {'x': dev_x, 'y': dev_y, 'c': dev_c}[route]
        return pltpu.make_async_remote_copy(dst, dst, w_send.at[k - 1, hop], w_recv.at[k - 1, hop], device_id=dev, device_id_type=MESH)

    own_slices = [pltpu.make_async_copy(wz_hbm.at[peer_shard(tp, k)], w_v.at[k, rows_of(dp, cp)], own_sem.at[k - 1]) for k in (1, 2, 3)]
    for k in (1, 2, 3):
        w_copy(k, 0).start()
        w_copy(k, 3).start()
        w_copy(k, 6).start()
        own_slices[k - 1].start()
    for k in (1, 2, 3):
        w_copy(k, 1).start()
        w_copy(k, 4).start()

    n_tile = 512

    def multiply(k, c, store):
        shard = tp if k == 0 else peer_shard(tp, k)
        lhs = o_v[shard, piece(c), :]

        @pl.loop(0, n_cols // n_tile)
        def _(n):
            out = pl.ds(pl.multiple_of(n * n_tile, n_tile), n_tile)
            part = jnp.dot(lhs, w_v[k, :, out], preferred_element_type=F32)
            store(out, part)

    own_w.wait()
    own_o.wait()

    @pl.loop(0, n_pc)
    def _(c):
        def store(out, part):
            acc_v[piece(c), out] = part

        multiply(0, c, store)

    for k in (1, 2, 3):
        w_arrival(k, 0).wait_recv()
        w_copy(k, 5).start()
        w_copy(k, 7).start()
        w_arrival(k, 3).wait_recv()
        w_copy(k, 2).start()
        w_copy(k, 10).start()

    @pl.loop(0, n_pc)
    def _(c):
        o_forward(1, c)

        @pl.when(mid == 1)
        def _():
            o_forward(3, c)

    for k in (1, 2, 3):
        w_arrival(k, 1).wait_recv()
        w_copy(k, 8).start()
        w_arrival(k, 4).wait_recv()
        w_copy(k, 11).start()

    def w_finish(k):
        w_arrival(k, 2).wait_recv()
        w_copy(k, 9).start()
        w_arrival(k, 5).wait_recv()
        w_copy(k, 12).start()
        for hop in range(6, 13):
            w_arrival(k, hop).wait_recv()
        own_slices[k - 1].wait()

    w_finish(1)

    @pl.loop(0, n_pc)
    def _(c):
        def store(out, part):
            acc_v[piece(c), out] += part

        multiply(1, c, store)

    w_finish(2)

    @pl.loop(0, n_pc)
    def _(c):
        def store(out, part):
            acc_v[piece(c), out] += part

        o_forward(2, c)
        multiply(2, c, store)

    w_finish(3)

    def y_copy(slot, c):
        return pltpu.make_async_copy(y_v.at[slot], y_hbm.at[piece(c)], y_sem.at[slot])

    @pl.loop(0, n_pc)
    def _(c):
        slot = lax.rem(c, 2)
        pl.when(mid == 0)(lambda: o_next(3, c).wait_recv())
        pl.when(c >= 2)(lambda: y_copy(slot, c - 2).wait())

        def store(out, part):
            y_v[slot, :, out] = (acc_v[piece(c), out] + part).astype(BF16)

        multiply(3, c, store)
        y_copy(slot, c).start()

    for c in (n_pc - 2, n_pc - 1):
        y_copy(c % 2, c).wait()
    for k in (1, 2, 3):
        for hop in range(len(hops)):
            w_copy(k, hop).wait_send()

    @pl.loop(0, n_pc)
    def _(c):
        pl.when(tp < 3)(lambda: o_up(c).wait_send())
        pl.when(tp > 0)(lambda: o_down(c).wait_send())

        @pl.when(mid == 1)
        def _():
            for k in (1, 2, 3):
                o_next(k, c).wait_send()


def solution(mesh):
    any_spec = pl.BlockSpec(memory_space=pl.ANY)
    vmem_spec = pl.BlockSpec(memory_space=pltpu.VMEM)
    dma = pltpu.SemaphoreType.DMA

    def layer(x_loc, seg_loc, w_query, w_key, w_value, w_out):
        chunk, width = x_loc.shape
        q_cols = w_query.shape[1]
        n_rows = w_out.shape[0] // 8
        n_blk = chunk // Q_BLK
        seg_col = jnp.broadcast_to(seg_loc[:, None], (chunk, HEAD_DIM))
        seg_row = jnp.broadcast_to(seg_loc[None, :], (8, chunk))
        heads_out, w_slices = pl.pallas_call(
            attend_kernel,
            name='attend',
            out_shape=(jax.ShapeDtypeStruct((chunk, q_cols), BF16), jax.ShapeDtypeStruct((4, n_rows, w_out.shape[1]), BF16)),
            in_specs=[any_spec, vmem_spec, any_spec, any_spec, any_spec, any_spec, any_spec],
            out_specs=(vmem_spec, any_spec),
            scratch_shapes=[
                pltpu.VMEM((chunk, width), BF16),
                pltpu.VMEM((width, q_cols), BF16),
                pltpu.VMEM((width, 2 * HEAD_DIM), BF16),
                pltpu.VMEM((chunk, q_cols), BF16),
                pltpu.VMEM((4 * chunk, 2 * HEAD_DIM), BF16),
                pltpu.VMEM((8, 4 * chunk), jnp.int32),
                pltpu.VMEM((Q_BLK, chunk), F32),
                pltpu.VMEM((chunk, q_cols), F32),
                pltpu.VMEM((chunk, q_cols), F32),
                pltpu.VMEM((chunk, q_cols), F32),
                dma((n_blk + 4,)), dma((3,)), dma((3,)), dma((3,)), dma((3,)), dma((5,)), dma((4,)),
            ],
            compiler_params=pltpu.CompilerParams(collective_id=0, has_side_effects=True, vmem_limit_bytes=62 << 20),
        )(x_loc, seg_col, seg_row, w_query, w_key, w_value, w_out)
        n_pc = chunk // O_ROWS
        return pl.pallas_call(
            output_kernel,
            name='output',
            out_shape=jax.ShapeDtypeStruct((chunk, w_out.shape[1]), BF16),
            in_specs=[any_spec, any_spec, any_spec],
            out_specs=any_spec,
            scratch_shapes=[
                pltpu.VMEM((4,) + w_out.shape, BF16),
                pltpu.VMEM((4, chunk, q_cols), BF16),
                pltpu.VMEM((chunk, w_out.shape[1]), F32),
                pltpu.VMEM((2, O_ROWS, w_out.shape[1]), BF16),
                dma((2,)), dma((3,)), dma((3, 13)), dma((3, 13)), dma((5, n_pc)), dma((4, n_pc)), dma((2,)),
            ],
            compiler_params=pltpu.CompilerParams(collective_id=1, has_side_effects=True, vmem_limit_bytes=62 << 20),
        )(heads_out, w_out, w_slices)

    return jax.shard_map(layer, mesh=mesh, in_specs=(P(('dp', 'cp'), None), P(('dp', 'cp')), P(None, 'tp'), P(None, 'tp'), P(None, 'tp'), P('tp', None)), out_specs=P(('dp', 'cp'), None), check_vma=False)
```

time: 692 us -> 250 us (0.36)
  the two profiles are of different devices: /device:TPU:6 before, /device:TPU:0 now
where the time goes in v1:
time: 250 us
  Pallas kernels  240 us (96%)
  local copies, waits for them, and re-layouts  9.59 us (4%)
    pallas_call x1, Pallas kernels, layer(): pl.pallas_call(output_kernel, name='output', out_shape=jax.ShapeDtypeStru...  167 us
    pallas_call x1, Pallas kernels, layer(): pl.pallas_call(attend_kernel, name='attend', out_shape=(jax.ShapeDtypeStr...  72.6 us
    unnamed x1, local copies, waits for them, and re-layouts  6.6 us

profile of v1, /device:TPU:0, one launch (start us, length us, event | category | flops | bytes accessed | tf_op | source)
XLA Modules:
  0.0 249.7 jit_solution(17862674899301701457)
XLA Ops:
  0.0 1.3 broadcast_in_dim.5.seg_row
  1.3 1.7 broadcast_in_dim.4.seg_col
  3.0 72.6 %attend.1 = (bf16[1024,896]{1,0:T(8,128)(2,1)}, bf16[4,112,3584]{2,1,0:T(8,128)(2,1)}) custom-call(bf16[1024,3584]{1,0:T(8,128)(2,1)} %x_hbm.1, s32[1024,128]{1,0:T(8,128)} %broadcast_in_dim.4.seg_col, s32[8,1024]{1,0:T(8,128)} %broadcast_in_dim.5.seg_row, bf16[3584,896]{1,0:T(8,128)(2,1)} %wq_hbm.1, bf16[3584,128]{1,0:T(8,128)(2,1)} %wk_hbm.1, ...), custom_call_target="tpu_custom_call" | custom-call | tf_op jit(solution)/shard_map/attend/pallas_call | solution.py:434
  75.6 167.4 %output.1 = bf16[1024,3584]{1,0:T(8,128)(2,1)} custom-call(bf16[1024,896]{1,0:T(8,128)(2,1)} %get-tuple-element.7.o_hbm, bf16[896,3584]{1,0:T(8,128)(2,1)} %wo_hbm.3, bf16[4,112,3584]{2,1,0:T(8,128)(2,1)} %get-tuple-element.8.wz_hbm), custom_call_target="tpu_custom_call" | custom-call | tf_op jit(solution)/shard_map/output/pallas_call | solution.py:456
  243.1 6.6 %copy.8 = bf16[1024,3584]{1,0:T(8,128)(2,1)} copy(bf16[1024,3584]{1,0:T(8,128)(2,1)} %output.1) | data formatting | bytes 14680064

commit v2 on v0

v2 whole, which is shorter than its diff:
```python
import functools

import jax
import jax.numpy as jnp
from jax import lax
from jax.experimental import pallas as pl
from jax.experimental.pallas import tpu as pltpu
from jax.sharding import PartitionSpec as P

HEAD_DIM = 128
MESH = pl.DeviceIdType.MESH
LOG2_SCALE = (HEAD_DIM ** -0.5) * 1.4426950408889634
F32 = jnp.float32
BF16 = jnp.bfloat16

Q_BLK = 256
LOC_BLK = 512
O_ROWS = 128


def coords():
    return lax.axis_index('dp'), lax.axis_index('tp'), lax.axis_index('cp')


def greet(dp, tp, cp, mid):
    bar = pltpu.get_barrier_semaphore()

    def hello(dev):
        pl.semaphore_signal(bar, inc=1, device_id=dev, device_id_type=MESH)

    hello((1 - dp, tp, cp))
    hello((dp, tp, lax.rem(cp + 2, 4)))
    hello((dp, tp, cp + 1 - 2 * lax.rem(cp, 2)))
    pl.when(tp > 0)(lambda: hello((dp, tp - 1, cp)))
    pl.when(tp < 3)(lambda: hello((dp, tp + 1, cp)))
    pl.semaphore_wait(bar, 4 + mid)


def peer_shard(tp, k):
    if k == 1:
        return tp + 1 - 2 * lax.rem(tp, 2)
    if k == 2:
        return lax.rem(tp + 2, 4)
    return 3 - tp


def layer_kernel(x_hbm, seg_hbm, wq_hbm, wk_hbm, wv_hbm, wo_hbm, y_hbm,
                 w_v, o_v, kv_v, seg_v,
                 load_sem, kv_send, kv_recv, seg_send, seg_recv, z_send, z_recv, w_send, w_recv, o_send, o_recv, y_sem):
    dp, tp, cp = coords()
    mid = lax.rem((tp + 1) // 2, 2)
    core = lax.rem(cp, 2)
    chunk, d_model = x_hbm.shape
    q_cols = wq_hbm.shape[1]
    heads = q_cols // HEAD_DIM
    n_rows = wo_hbm.shape[0] // 8
    n_cols = wo_hbm.shape[1]
    half = n_cols // 2
    n_blk = chunk // Q_BLK
    n_pc = chunk // O_ROWS
    per_blk = Q_BLK // O_ROWS
    cp_y = lax.rem(cp + 2, 4)
    cp_c = cp + 1 - 2 * core
    dev_x, dev_y, dev_c = (1 - dp, tp, cp), (dp, tp, cp_y), (dp, tp, cp_c)

    def onward(shard):
        return tp + 1 - 2 * (shard // (tp + 1) > 0).astype(jnp.int32)

    def rows_of(dp_i, cp_i):
        return pl.ds(pl.multiple_of((dp_i * 4 + cp_i) * n_rows, 16), n_rows)

    def z_copy(slot, src, shard, to):
        return pltpu.make_async_remote_copy(src, w_v.at[shard, rows_of(dp, cp)], z_send.at[slot], z_recv.at[shard],
                                            device_id=(dp, to, cp), device_id_type=MESH)

    z_up = z_copy(0, wo_hbm.at[rows_of(dp, cp)], tp, tp + 1)
    z_down = z_copy(4, wo_hbm.at[rows_of(dp, cp)], tp, tp - 1)

    def z_next(k):
        shard = peer_shard(tp, k)
        return z_copy(k, w_v.at[shard, rows_of(dp, cp)], shard, onward(shard))

    cuts = {'a': pl.ds(0, half), 'b': pl.ds(half, half), 'ab': pl.ds(0, n_cols)}
    hops = [('x', 'own', 'a'), ('x', 'own', 'b'), ('x', 'y', 'b'), ('y', 'own', 'b'), ('y', 'own', 'a'), ('y', 'x', 'a'),
            ('c', 'own', 'ab'), ('c', 'x', 'a'), ('c', 'x', 'b'), ('c', 'd', 'b'), ('c', 'y', 'b'), ('c', 'y', 'a'), ('c', 'd', 'a')]

    def slice_rows(name, dp_i, cp_i):
        far = lax.rem(cp_i + 2, 4)
        return {'own': rows_of(dp_i, cp_i), 'x': rows_of(1 - dp_i, cp_i), 'y': rows_of(dp_i, far), 'd': rows_of(1 - dp_i, far)}[name]

    def w_hop(k, hop, dp_i, cp_i):
        route, name, part = hops[hop]
        at = w_v.at[peer_shard(tp, k), slice_rows(name, dp_i, cp_i), cuts[part]]
        dev = {'x': dev_x, 'y': dev_y, 'c': dev_c}[route]
        return pltpu.make_async_remote_copy(at, at, w_send.at[k - 1, hop], w_recv.at[k - 1, hop], device_id=dev, device_id_type=MESH)

    def w_copy(k, hop):
        return w_hop(k, hop, dp, cp)

    def w_arrival(k, hop):
        dp_i, cp_i = {'x': (1 - dp, cp), 'y': (dp, cp_y), 'c': (dp, cp_c)}[hops[hop][0]]
        return w_hop(k, hop, dp_i, cp_i)

    def w_enter(k):
        z_next(k).wait_recv()
        pl.when(mid == 1)(lambda: z_next(k).start())
        for hop in (0, 3, 6, 1, 4):
            w_copy(k, hop).start()

    def piece(c):
        return pl.ds(pl.multiple_of(c * O_ROWS, O_ROWS), O_ROWS)

    def o_copy(slot, c, shard, to):
        at = o_v.at[shard, piece(c)]
        return pltpu.make_async_remote_copy(at, at, o_send.at[slot, c], o_recv.at[shard, c], device_id=(dp, to, cp), device_id_type=MESH)

    def o_up(c):
        return o_copy(0, c, tp, tp + 1)

    def o_down(c):
        return o_copy(4, c, tp, tp - 1)

    def o_leave(i):
        for j in range(per_blk):
            pl.when(tp < 3)(lambda: o_up(i * per_blk + j).start())
            pl.when(tp > 0)(lambda: o_down(i * per_blk + j).start())

    def o_next(k, c):
        shard = peer_shard(tp, k)
        return o_copy(k, c, shard, onward(shard))

    def o_forward(k, c):
        o_next(k, c).wait_recv()
        pl.when(mid == 1)(lambda: o_next(k, c).start())

    def kv_copies(slot, block, to):
        rows = pl.ds(pl.multiple_of(block * chunk, chunk), chunk)
        dev = (dp, tp, to)
        return (pltpu.make_async_remote_copy(kv_v.at[rows], kv_v.at[rows], kv_send.at[slot], kv_recv.at[slot],
                                             device_id=dev, device_id_type=MESH),
                pltpu.make_async_remote_copy(seg_v.at[:, rows], seg_v.at[:, rows], seg_send.at[slot], seg_recv.at[slot],
                                             device_id=dev, device_id_type=MESH))

    def over(copies, what):
        for copy in copies:
            getattr(copy, what)()

    own_w = pltpu.make_async_copy(wo_hbm, w_v.at[tp], load_sem.at[n_blk + 4])

    def attend(x_v, wq_v, wkv_v, q_v, col_v, bias_v, m_v, l_v, acc_v):
        loads = []
        for i in range(n_blk):
            rows = slice(i * Q_BLK, (i + 1) * Q_BLK)
            loads.append(pltpu.make_async_copy(x_hbm.at[rows], x_v.at[rows], load_sem.at[i]))
        k_load = pltpu.make_async_copy(wk_hbm, wkv_v.at[:, 0:HEAD_DIM], load_sem.at[n_blk])
        v_load = pltpu.make_async_copy(wv_hbm, wkv_v.at[:, HEAD_DIM:2 * HEAD_DIM], load_sem.at[n_blk + 1])
        q_load = pltpu.make_async_copy(wq_hbm, wq_v, load_sem.at[n_blk + 2])
        own = pl.ds(pl.multiple_of(cp * chunk, chunk), chunk)
        seg_load = pltpu.make_async_copy(seg_hbm, seg_v.at[:, own], load_sem.at[n_blk + 3])
        k_load.start()
        v_load.start()
        for load in loads:
            load.start()
        q_load.start()
        seg_load.start()
        own_w.start()

        greet(dp, tp, cp, mid)
        pl.when(tp < 3)(z_up.start)
        pl.when(tp > 0)(z_down.start)

        k_load.wait()
        v_load.wait()
        for i in range(n_blk):
            loads[i].wait()
            rows = slice(i * Q_BLK, (i + 1) * Q_BLK)
            kv_v[pl.ds(pl.multiple_of(cp * chunk + i * Q_BLK, Q_BLK), Q_BLK), :] = jnp.dot(
                x_v[rows, :], wkv_v[...], preferred_element_type=F32).astype(BF16)

        q_load.wait()

        def project(i):
            rows = pl.ds(pl.multiple_of(i * Q_BLK, Q_BLK), Q_BLK)
            q_v[rows, :] = jnp.dot(x_v[rows, :], wq_v[...], preferred_element_type=F32).astype(BF16)

        project(0)
        seg_load.wait()
        pl.when(cp < 2)(lambda: over(kv_copies(0, cp, cp_y), 'start'))
        pl.when(core == 0)(lambda: over(kv_copies(1, cp, cp_c), 'start'))

        @pl.loop(1, n_blk)
        def _(i):
            project(i)

        @pl.loop(0, chunk // HEAD_DIM)
        def _(i):
            ids = seg_v[0:1, pl.ds(pl.multiple_of(cp * chunk + i * HEAD_DIM, HEAD_DIM), HEAD_DIM)]
            rows = pl.ds(pl.multiple_of(i * HEAD_DIM, HEAD_DIM), HEAD_DIM)
            col_v[rows, :] = jnp.transpose(jnp.broadcast_to(ids, (HEAD_DIM, HEAD_DIM)))

        w_enter(1)
        pl.when(mid == 1)(lambda: w_enter(3))

        @pl.when(cp >= 2)
        def _():
            over(kv_copies(0, cp - 2, cp), 'wait_recv')
            over(kv_copies(2, cp - 2, cp_c), 'start')
            over(kv_copies(2, cp_c - 2, cp), 'wait_recv')

        @pl.when(core == 1)
        def _():
            over(kv_copies(1, cp_c, cp), 'wait_recv')

        def step(i, key0, n_keys, first):
            rows = pl.ds(pl.multiple_of(i * Q_BLK, Q_BLK), Q_BLK)
            keys = pl.ds(pl.multiple_of(key0, n_keys), n_keys)
            groups = n_keys // HEAD_DIM
            q_seg = col_v[rows, :]
            for g in range(groups):
                cols = pl.ds(pl.multiple_of(key0 + g * HEAD_DIM, HEAD_DIM), HEAD_DIM)
                ok = q_seg == seg_v[0:1, cols]
                if first:
                    q_pos = cp * chunk + i * Q_BLK + lax.broadcasted_iota(jnp.int32, (Q_BLK, HEAD_DIM), 0)
                    k_pos = key0 + g * HEAD_DIM + lax.broadcasted_iota(jnp.int32, (Q_BLK, HEAD_DIM), 1)
                    ok = ok & (q_pos >= k_pos)
                bias_v[:, g * HEAD_DIM:(g + 1) * HEAD_DIM] = jnp.where(ok, 0.0, -jnp.inf)
            k_blk = kv_v[keys, 0:HEAD_DIM]
            v_blk = kv_v[keys, HEAD_DIM:2 * HEAD_DIM]
            for h in range(heads):
                cols = slice(h * HEAD_DIM, (h + 1) * HEAD_DIM)
                s = lax.dot_general(q_v[rows, cols], k_blk, (((1,), (1,)), ((), ())), preferred_element_type=F32)
                s = [s[:, g * HEAD_DIM:(g + 1) * HEAD_DIM] + bias_v[:, g * HEAD_DIM:(g + 1) * HEAD_DIM] for g in range(groups)]
                top = jnp.max(functools.reduce(jnp.maximum, s), axis=1, keepdims=True)
                if first:
                    m_new = jnp.broadcast_to(top, (Q_BLK, HEAD_DIM))
                else:
                    m_old = m_v[:, cols]
                    m_new = jnp.maximum(m_old, top)
                    fade = jnp.exp2((m_old - m_new) * LOG2_SCALE)
                p = [jnp.exp2((part - m_new) * LOG2_SCALE) for part in s]
                total = functools.reduce(jnp.add, p)
                probs = jnp.concatenate([part.astype(BF16) for part in p], axis=1)
                pv = jnp.dot(probs, v_blk, preferred_element_type=F32)
                m_v[:, cols] = m_new
                if first:
                    l_v[:, cols] = total
                    acc_v[:, cols] = pv
                else:
                    l_v[:, cols] = l_v[:, cols] * fade + total
                    acc_v[:, cols] = acc_v[:, cols] * fade + pv

        per_loc = LOC_BLK // Q_BLK

        @pl.loop(0, n_blk)
        def _(i):
            last = i // per_loc
            step(i, cp * chunk + last * LOC_BLK, LOC_BLK, True)
            pl.when(i > 0)(lambda: o_leave(i - 1))

            @pl.loop(0, last)
            def _(j):
                step(i, cp * chunk + j * LOC_BLK, LOC_BLK, False)

            @pl.loop(0, cp)
            def _(j):
                step(i, j * chunk, chunk, False)

            rows = pl.ds(pl.multiple_of(i * Q_BLK, Q_BLK), Q_BLK)
            for h in range(heads):
                cols = slice(h * HEAD_DIM, (h + 1) * HEAD_DIM)
                total = jnp.sum(l_v[:, cols], axis=1, keepdims=True)
                o_v[tp, rows, cols] = (acc_v[:, cols] / total).astype(BF16)

            pl.when(i == 0)(lambda: w_enter(2))

    pl.run_scoped(
        attend,
        pltpu.VMEM((chunk, d_model), BF16),
        pltpu.VMEM((d_model, q_cols), BF16),
        pltpu.VMEM((d_model, 2 * HEAD_DIM), BF16),
        pltpu.VMEM((chunk, q_cols), BF16),
        pltpu.VMEM((chunk, HEAD_DIM), jnp.int32),
        pltpu.VMEM((Q_BLK, chunk), F32),
        pltpu.VMEM((Q_BLK, q_cols), F32),
        pltpu.VMEM((Q_BLK, q_cols), F32),
        pltpu.VMEM((Q_BLK, q_cols), F32),
    )

    def output(acc_v, y_v):
        n_tile = 512

        def multiply(k, c, store):
            shard = tp if k == 0 else peer_shard(tp, k)
            lhs = o_v[shard, piece(c), :]

            @pl.loop(0, n_cols // n_tile)
            def _(n):
                out = pl.ds(pl.multiple_of(n * n_tile, n_tile), n_tile)
                store(out, jnp.dot(lhs, w_v[shard, :, out], preferred_element_type=F32))

        own_w.wait()

        @pl.loop(0, n_pc)
        def _(c):
            def store(out, part):
                acc_v[piece(c), out] = part

            multiply(0, c, store)
            pl.when(c == 0)(lambda: o_leave(n_blk - 1))

        pl.when(mid == 0)(lambda: w_enter(3))

        for k in (1, 2, 3):
            w_arrival(k, 0).wait_recv()
            w_copy(k, 5).start()
            w_copy(k, 7).start()
            w_arrival(k, 3).wait_recv()
            w_copy(k, 2).start()
            w_copy(k, 10).start()

        @pl.loop(0, n_pc)
        def _(c):
            o_forward(1, c)
            pl.when(mid == 1)(lambda: o_forward(3, c))

        for k in (1, 2, 3):
            w_arrival(k, 1).wait_recv()
            w_copy(k, 8).start()
            w_arrival(k, 4).wait_recv()
            w_copy(k, 11).start()

        def w_finish(k):
            w_arrival(k, 2).wait_recv()
            w_copy(k, 9).start()
            w_arrival(k, 5).wait_recv()
            w_copy(k, 12).start()
            for hop in range(6, 13):
                w_arrival(k, hop).wait_recv()

        w_finish(1)

        @pl.loop(0, n_pc)
        def _(c):
            def store(out, part):
                acc_v[piece(c), out] += part

            multiply(1, c, store)

        w_finish(2)

        @pl.loop(0, n_pc)
        def _(c):
            def store(out, part):
                acc_v[piece(c), out] += part

            o_forward(2, c)
            multiply(2, c, store)

        w_finish(3)

        def y_copy(slot, c):
            return pltpu.make_async_copy(y_v.at[slot], y_hbm.at[piece(c)], y_sem.at[slot])

        @pl.loop(0, n_pc)
        def _(c):
            slot = lax.rem(c, 2)
            pl.when(mid == 0)(lambda: o_next(3, c).wait_recv())
            pl.when(c >= 2)(lambda: y_copy(slot, c - 2).wait())

            def store(out, part):
                y_v[slot, :, out] = (acc_v[piece(c), out] + part).astype(BF16)

            multiply(3, c, store)
            y_copy(slot, c).start()

        for c in (n_pc - 2, n_pc - 1):
            y_copy(c % 2, c).wait()

    pl.run_scoped(output, pltpu.VMEM((chunk, n_cols), F32), pltpu.VMEM((2, O_ROWS, n_cols), BF16))

    pl.when(cp < 2)(lambda: over(kv_copies(0, cp, cp_y), 'wait_send'))
    pl.when(core == 0)(lambda: over(kv_copies(1, cp, cp_c), 'wait_send'))
    pl.when(cp >= 2)(lambda: over(kv_copies(2, cp - 2, cp_c), 'wait_send'))
    pl.when(tp < 3)(z_up.wait_send)
    pl.when(tp > 0)(z_down.wait_send)
    for k in (1, 2, 3):
        pl.when(mid == 1)(lambda: z_next(k).wait_send())
        for hop in range(len(hops)):
            w_copy(k, hop).wait_send()

    @pl.loop(0, n_pc)
    def _(c):
        pl.when(tp < 3)(lambda: o_up(c).wait_send())
        pl.when(tp > 0)(lambda: o_down(c).wait_send())

        @pl.when(mid == 1)
        def _():
            for k in (1, 2, 3):
                o_next(k, c).wait_send()


def solution(mesh):
    any_spec = pl.BlockSpec(memory_space=pl.ANY)
    dma = pltpu.SemaphoreType.DMA

    def layer(x_loc, seg_loc, w_query, w_key, w_value, w_out):
        chunk = x_loc.shape[0]
        q_cols = w_query.shape[1]
        n_blk = chunk // Q_BLK
        n_pc = chunk // O_ROWS
        return pl.pallas_call(
            layer_kernel,
            name='layer',
            out_shape=jax.ShapeDtypeStruct((chunk, w_out.shape[1]), BF16),
            in_specs=[any_spec] * 6,
            out_specs=any_spec,
            scratch_shapes=[
                pltpu.VMEM((4,) + w_out.shape, BF16),
                pltpu.VMEM((4, chunk, q_cols), BF16),
                pltpu.VMEM((4 * chunk, 2 * HEAD_DIM), BF16),
                pltpu.VMEM((1, 4 * chunk), jnp.int32),
                dma((n_blk + 5,)), dma((3,)), dma((3,)), dma((3,)), dma((3,)), dma((5,)), dma((4,)),
                dma((3, 13)), dma((3, 13)), dma((5, n_pc)), dma((4, n_pc)), dma((2,)),
            ],
            compiler_params=pltpu.CompilerParams(collective_id=0, has_side_effects=True, vmem_limit_bytes=67043328),
        )(x_loc, seg_loc[None, :], w_query, w_key, w_value, w_out)

    return jax.shard_map(layer, mesh=mesh, in_specs=(P(('dp', 'cp'), None), P(('dp', 'cp')), P(None, 'tp'), P(None, 'tp'), P(None, 'tp'), P('tp', None)), out_specs=P(('dp', 'cp'), None), check_vma=False)
```

time: 692 us -> 196 us (0.28)
  the two profiles are of different devices: /device:TPU:6 before, /device:TPU:0 now
where the time goes in v2:
time: 196 us
  Pallas kernels  190 us (97%)
  local copies, waits for them, and re-layouts  6.6 us (3%)
    pallas_call x1, Pallas kernels, layer(): pl.pallas_call(layer_kernel, name='layer', out_shape=jax.ShapeDtypeStruct...  190 us
    unnamed x1, local copies, waits for them, and re-layouts  6.6 us

profile of v2, /device:TPU:0, one launch (start us, length us, event | category | flops | bytes accessed | tf_op | source)
XLA Modules:
  0.0 196.1 jit_solution(14085311665271650770)
XLA Ops:
  0.0 189.5 %layer.1 = bf16[1024,3584]{1,0:T(8,128)(2,1)} custom-call(bf16[1024,3584]{1,0:T(8,128)(2,1)} %x_hbm.1, s32[1,1024]{1,0:T(1,128)} %bitcast.1, bf16[3584,896]{1,0:T(8,128)(2,1)} %wq_hbm.1, bf16[3584,128]{1,0:T(8,128)(2,1)} %wk_hbm.1, bf16[3584,128]{1,0:T(8,128)(2,1)} %wv_hbm.1, bf16[896,3584]{1,0:T(8,128)(2,1)} %wo_hbm.1), custom_call_target="tpu_custom_call" | custom-call | tf_op jit(solution)/shard_map/layer/pallas_call | solution.py:411
  189.5 6.6 %copy.8 = bf16[1024,3584]{1,0:T(8,128)(2,1)} copy(bf16[1024,3584]{1,0:T(8,128)(2,1)} %layer.1) | data formatting | bytes 14680064

commit v3 on v2

v3 whole, which is shorter than its diff:
```python
import functools

import jax
import jax.numpy as jnp
from jax import lax
from jax.experimental import pallas as pl
from jax.experimental.pallas import tpu as pltpu
from jax.sharding import PartitionSpec as P

HEAD_DIM = 128
MESH = pl.DeviceIdType.MESH
LOG2_SCALE = (HEAD_DIM ** -0.5) * 1.4426950408889634
F32 = jnp.float32
BF16 = jnp.bfloat16

Q_BLK = 256
LOC_BLK = 512
O_ROWS = 128


def coords():
    return lax.axis_index('dp'), lax.axis_index('tp'), lax.axis_index('cp')


def greet(dp, tp, cp, mid):
    bar = pltpu.get_barrier_semaphore()

    def hello(dev):
        pl.semaphore_signal(bar, inc=1, device_id=dev, device_id_type=MESH)

    hello((1 - dp, tp, cp))
    hello((dp, tp, lax.rem(cp + 2, 4)))
    hello((dp, tp, cp + 1 - 2 * lax.rem(cp, 2)))
    pl.when(tp > 0)(lambda: hello((dp, tp - 1, cp)))
    pl.when(tp < 3)(lambda: hello((dp, tp + 1, cp)))
    pl.semaphore_wait(bar, 4 + mid)


def peer_shard(tp, k):
    if k == 1:
        return tp + 1 - 2 * lax.rem(tp, 2)
    if k == 2:
        return lax.rem(tp + 2, 4)
    return 3 - tp


def layer_kernel(x_hbm, seg_hbm, wq_hbm, wk_hbm, wv_hbm, wo_hbm, y_hbm,
                 w_v, o_v, kv_v, seg_v, wx_v,
                 load_sem, kv_send, kv_recv, seg_send, seg_recv, x_send, x_recv, z_send, z_recv, w_send, w_recv, o_send, o_recv, y_sem):
    dp, tp, cp = coords()
    mid = lax.rem((tp + 1) // 2, 2)
    core = lax.rem(cp, 2)
    chunk, d_model = x_hbm.shape
    q_cols = wq_hbm.shape[1]
    heads = q_cols // HEAD_DIM
    n_rows = wo_hbm.shape[0] // 8
    n_cols = wo_hbm.shape[1]
    half = n_cols // 2
    x_rows = d_model // 8
    wx_cols = q_cols + 2 * HEAD_DIM
    n_blk = chunk // Q_BLK
    n_pc = chunk // O_ROWS
    per_blk = Q_BLK // O_ROWS
    cp_y = lax.rem(cp + 2, 4)
    cp_c = cp + 1 - 2 * core
    dev_x, dev_y, dev_c = (1 - dp, tp, cp), (dp, tp, cp_y), (dp, tp, cp_c)

    def onward(shard):
        return tp + 1 - 2 * (shard // (tp + 1) > 0).astype(jnp.int32)

    def rows_of(dp_i, cp_i):
        return pl.ds(pl.multiple_of((dp_i * 4 + cp_i) * n_rows, 16), n_rows)

    def z_copy(slot, src, shard, to):
        return pltpu.make_async_remote_copy(src, w_v.at[shard, rows_of(dp, cp)], z_send.at[slot], z_recv.at[shard],
                                            device_id=(dp, to, cp), device_id_type=MESH)

    z_up = z_copy(0, wo_hbm.at[rows_of(dp, cp)], tp, tp + 1)
    z_down = z_copy(4, wo_hbm.at[rows_of(dp, cp)], tp, tp - 1)

    def z_next(k):
        shard = peer_shard(tp, k)
        return z_copy(k, w_v.at[shard, rows_of(dp, cp)], shard, onward(shard))

    def x_slice(dp_i, cp_i, part='ab'):
        first = (dp_i * 4 + cp_i) * x_rows + (x_rows // 2 if part == 'b' else 0)
        return pl.ds(pl.multiple_of(first, 16), x_rows if part == 'ab' else x_rows // 2)

    def wx_copies():
        rows = x_slice(dp, cp)
        out = []
        for n, (src, lo, hi) in enumerate(((wq_hbm, 0, q_cols), (wk_hbm, q_cols, q_cols + HEAD_DIM), (wv_hbm, q_cols + HEAD_DIM, wx_cols))):
            out.append(pltpu.make_async_remote_copy(src.at[rows], wx_v.at[rows, lo:hi], x_send.at[n], x_recv.at[n],
                                                    device_id=(dp, tp - 1 + 2 * (tp // 2), cp), device_id_type=MESH))
        return out

    cuts = {'a': pl.ds(0, half), 'b': pl.ds(half, half), 'ab': pl.ds(0, n_cols)}
    hops = [('x', 'own', 'a'), ('x', 'own', 'b'), ('x', 'y', 'b'), ('y', 'own', 'b'), ('y', 'own', 'a'), ('y', 'x', 'a'),
            ('c', 'own', 'ab'), ('c', 'x', 'a'), ('c', 'x', 'b'), ('c', 'd', 'b'), ('c', 'y', 'b'), ('c', 'y', 'a'), ('c', 'd', 'a')]

    def holder(name, dp_i, cp_i):
        far = lax.rem(cp_i + 2, 4)
        return {'own': (dp_i, cp_i), 'x': (1 - dp_i, cp_i), 'y': (dp_i, far), 'd': (1 - dp_i, far)}[name]

    def w_hop(k, hop, dp_i, cp_i):
        route, name, part = hops[hop]
        if k == 4:
            at = wx_v.at[x_slice(*holder(name, dp_i, cp_i), part)]
        else:
            at = w_v.at[peer_shard(tp, k), rows_of(*holder(name, dp_i, cp_i)), cuts[part]]
        dev = {'x': dev_x, 'y': dev_y, 'c': dev_c}[route]
        return pltpu.make_async_remote_copy(at, at, w_send.at[k - 1, hop], w_recv.at[k - 1, hop], device_id=dev, device_id_type=MESH)

    def w_copy(k, hop):
        return w_hop(k, hop, dp, cp)

    def w_arrival(k, hop):
        dp_i, cp_i = {'x': (1 - dp, cp), 'y': (dp, cp_y), 'c': (dp, cp_c)}[hops[hop][0]]
        return w_hop(k, hop, dp_i, cp_i)

    def w_enter(k):
        z_next(k).wait_recv()
        pl.when(mid == 1)(lambda: z_next(k).start())
        w_spread(k)

    def w_spread(k):
        for hop in (0, 3, 6, 1, 4):
            w_copy(k, hop).start()

    def w_pass_first(k):
        w_arrival(k, 0).wait_recv()
        w_copy(k, 5).start()
        w_copy(k, 7).start()
        w_arrival(k, 3).wait_recv()
        w_copy(k, 2).start()
        w_copy(k, 10).start()

    def w_pass_second(k):
        w_arrival(k, 1).wait_recv()
        w_copy(k, 8).start()
        w_arrival(k, 4).wait_recv()
        w_copy(k, 11).start()

    def w_finish(k):
        w_arrival(k, 2).wait_recv()
        w_copy(k, 9).start()
        w_arrival(k, 5).wait_recv()
        w_copy(k, 12).start()
        for hop in range(6, 13):
            w_arrival(k, hop).wait_recv()

    def piece(c):
        return pl.ds(pl.multiple_of(c * O_ROWS, O_ROWS), O_ROWS)

    def o_copy(slot, c, shard, to):
        at = o_v.at[shard, piece(c)]
        return pltpu.make_async_remote_copy(at, at, o_send.at[slot, c], o_recv.at[shard, c], device_id=(dp, to, cp), device_id_type=MESH)

    def o_own(c):
        return o_copy(0, c, tp, tp + 1 - 2 * (tp // 2))

    def o_leave(i):
        for j in range(per_blk):
            o_own(i * per_blk + j).start()

    def o_next(k, c):
        shard = peer_shard(tp, k)
        return o_copy(k, c, shard, onward(shard))

    def o_forward(k, c):
        o_next(k, c).wait_recv()
        pl.when(mid == 1)(lambda: o_next(k, c).start())

    def kv_copies(g, slot, block, to):
        rows = pl.ds(pl.multiple_of(block * chunk, chunk), chunk)
        dev = (dp, tp, to)
        kv = pltpu.make_async_remote_copy(kv_v.at[g, rows], kv_v.at[g, rows], kv_send.at[g, slot], kv_recv.at[g, slot],
                                          device_id=dev, device_id_type=MESH)
        if g == 1:
            return (kv,)
        return (kv, pltpu.make_async_remote_copy(seg_v.at[:, rows], seg_v.at[:, rows], seg_send.at[slot], seg_recv.at[slot],
            device_id=dev, device_id_type=MESH))

    def kv_leave(g):
        pl.when(cp < 2)(lambda: over(kv_copies(g, 0, cp, cp_y), 'start'))
        pl.when(core == 0)(lambda: over(kv_copies(g, 1, cp, cp_c), 'start'))

    def kv_wait(g):
        @pl.when(cp >= 2)
        def _():
            over(kv_copies(g, 0, cp - 2, cp), 'wait_recv')
            over(kv_copies(g, 2, cp - 2, cp_c), 'start')
            over(kv_copies(g, 2, cp_c - 2, cp), 'wait_recv')

        @pl.when(core == 1)
        def _():
            over(kv_copies(g, 1, cp_c, cp), 'wait_recv')

    def kv_sent(g):
        pl.when(cp < 2)(lambda: over(kv_copies(g, 0, cp, cp_y), 'wait_send'))
        pl.when(core == 0)(lambda: over(kv_copies(g, 1, cp, cp_c), 'wait_send'))
        pl.when(cp >= 2)(lambda: over(kv_copies(g, 2, cp - 2, cp_c), 'wait_send'))

    def over(copies, what):
        for copy in copies:
            getattr(copy, what)()

    own_w = pltpu.make_async_copy(wo_hbm, w_v.at[tp], load_sem.at[n_blk + 5])

    def attend(x_v, w_blk, q_v, col_v, bias_v, m_v, l_v, acc_v):
        n_w = 2 * HEAD_DIM
        own = pl.ds(pl.multiple_of(cp * chunk, chunk), chunk)
        x_loads = []
        for i in range(n_blk):
            rows = slice(i * Q_BLK, (i + 1) * Q_BLK)
            x_loads.append(pltpu.make_async_copy(x_hbm.at[rows], x_v.at[rows], load_sem.at[i]))
        seg_load = pltpu.make_async_copy(seg_hbm, seg_v.at[:, own], load_sem.at[n_blk])
        spans = [(lo, min(lo + n_w, q_cols)) for lo in range(0, q_cols, n_w)]
        w_loads = [[pltpu.make_async_copy(wk_hbm, w_blk.at[0, :, 0:HEAD_DIM], load_sem.at[n_blk + 1]),
                    pltpu.make_async_copy(wv_hbm, w_blk.at[0, :, HEAD_DIM:n_w], load_sem.at[n_blk + 2])]]
        for n, (lo, hi) in enumerate(spans):
            w_loads.append([pltpu.make_async_copy(wq_hbm.at[:, lo:hi], w_blk.at[(n + 1) % 2, :, 0:hi - lo],
                                                  load_sem.at[n_blk + 3 + (n + 1) % 2])])
        over(w_loads[0], 'start')
        over(x_loads, 'start')
        over(w_loads[1], 'start')
        seg_load.start()

        greet(dp, tp, cp, mid)
        pl.when(mid == 1)(lambda: over(wx_copies(), 'start'))
        pl.when(tp < 3)(z_up.start)
        pl.when(tp > 0)(z_down.start)

        def blk(i):
            return pl.ds(pl.multiple_of(i * Q_BLK, Q_BLK), Q_BLK)

        def own_rows(i):
            return pl.ds(pl.multiple_of(cp * chunk + i * Q_BLK, Q_BLK), Q_BLK)

        def product(i, w):
            return jnp.dot(x_v[blk(i), :], w, preferred_element_type=F32).astype(BF16)

        over(w_loads[0], 'wait')
        for i in range(n_blk):
            x_loads[i].wait()
            kv_v[0, own_rows(i), :] = product(i, w_blk[0])
        over(w_loads[2], 'start')
        seg_load.wait()
        for n, (lo, hi) in enumerate(spans):
            over(w_loads[n + 1], 'wait')

            @pl.loop(0, n_blk)
            def _(i):
                q_v[blk(i), lo:hi] = product(i, w_blk[(n + 1) % 2, :, 0:hi - lo])

            if n + 3 < len(w_loads):
                over(w_loads[n + 3], 'start')
            if n == 0:
                kv_leave(0)
        own_w.start()

        @pl.loop(0, chunk // HEAD_DIM)
        def _(i):
            ids = seg_v[0:1, pl.ds(pl.multiple_of(cp * chunk + i * HEAD_DIM, HEAD_DIM), HEAD_DIM)]
            rows = pl.ds(pl.multiple_of(i * HEAD_DIM, HEAD_DIM), HEAD_DIM)
            col_v[rows, :] = jnp.transpose(jnp.broadcast_to(ids, (HEAD_DIM, HEAD_DIM)))

        @pl.when(mid == 1)
        def _():
            w_enter(1)
            w_enter(3)

        @pl.when(mid == 0)
        def _():
            over(wx_copies(), 'wait_recv')
            w_spread(4)

        def step(g, i, key0, n_keys, first):
            keys = pl.ds(pl.multiple_of(key0, n_keys), n_keys)
            groups = n_keys // HEAD_DIM
            q_seg = col_v[blk(i), :]
            for n in range(groups):
                cols = pl.ds(pl.multiple_of(key0 + n * HEAD_DIM, HEAD_DIM), HEAD_DIM)
                ok = q_seg == seg_v[0:1, cols]
                if first:
                    q_pos = cp * chunk + i * Q_BLK + lax.broadcasted_iota(jnp.int32, (Q_BLK, HEAD_DIM), 0)
                    k_pos = key0 + n * HEAD_DIM + lax.broadcasted_iota(jnp.int32, (Q_BLK, HEAD_DIM), 1)
                    ok = ok & (q_pos >= k_pos)
                bias_v[:, n * HEAD_DIM:(n + 1) * HEAD_DIM] = jnp.where(ok, 0.0, -jnp.inf)
            k_blk = kv_v[g, keys, 0:HEAD_DIM]
            v_blk = kv_v[g, keys, HEAD_DIM:2 * HEAD_DIM]

            def scores(h):
                return lax.dot_general(q_v[blk(i), h * HEAD_DIM:(h + 1) * HEAD_DIM], k_blk, (((1,), (1,)), ((), ())),
                                       preferred_element_type=F32)

            ahead = scores(0)
            for h in range(heads):
                cols = slice(h * HEAD_DIM, (h + 1) * HEAD_DIM)
                s = ahead
                if h + 1 < heads:
                    ahead = scores(h + 1)
                s = [s[:, n * HEAD_DIM:(n + 1) * HEAD_DIM] + bias_v[:, n * HEAD_DIM:(n + 1) * HEAD_DIM] for n in range(groups)]
                top = jnp.max(functools.reduce(jnp.maximum, s), axis=1, keepdims=True)
                if first:
                    m_new = jnp.broadcast_to(top, (Q_BLK, HEAD_DIM))
                else:
                    m_old = m_v[:, cols]
                    m_new = jnp.maximum(m_old, top)
                    fade = jnp.exp2((m_old - m_new) * LOG2_SCALE)
                p = [jnp.exp2((part - m_new) * LOG2_SCALE) for part in s]
                total = functools.reduce(jnp.add, p)
                probs = jnp.concatenate([part.astype(BF16) for part in p], axis=1)
                pv = jnp.dot(probs, v_blk, preferred_element_type=F32)
                m_v[:, cols] = m_new
                if first:
                    l_v[:, cols] = total
                    acc_v[:, cols] = pv
                else:
                    l_v[:, cols] = l_v[:, cols] * fade + total
                    acc_v[:, cols] = acc_v[:, cols] * fade + pv

        per_loc = LOC_BLK // Q_BLK

        def attention(g, shard, after_first, after_block):
            @pl.loop(0, n_blk)
            def _(i):
                last = i // per_loc
                step(g, i, cp * chunk + last * LOC_BLK, LOC_BLK, True)
                after_first(i)

                @pl.loop(0, last)
                def _(j):
                    step(g, i, cp * chunk + j * LOC_BLK, LOC_BLK, False)

                pl.when(i == 0)(lambda: kv_wait(g))

                @pl.loop(0, cp)
                def _(j):
                    step(g, i, j * chunk, chunk, False)

                for h in range(heads):
                    cols = slice(h * HEAD_DIM, (h + 1) * HEAD_DIM)
                    total = jnp.sum(l_v[:, cols], axis=1, keepdims=True)
                    o_v[shard, blk(i), cols] = (acc_v[:, cols] / total).astype(BF16)
                after_block(i)

        def own_after_first(i):
            pl.when(i > 0)(lambda: o_leave(i - 1))

        def own_after_block(i):
            pl.when((i == 0) & (mid == 1))(lambda: w_enter(2))
            pl.when((i == 0) & (mid == 0))(lambda: w_pass_first(4))
            pl.when((i == 1) & (mid == 0))(lambda: w_enter(1))
            pl.when((i == 2) & (mid == 0))(lambda: w_pass_second(4))

        attention(0, tp, own_after_first, own_after_block)

        @pl.when(mid == 0)
        def _():
            w_finish(4)
            w_enter(2)

            @pl.loop(0, n_blk)
            def _(i):
                kv_v[1, own_rows(i), :] = product(i, wx_v[:, q_cols:wx_cols])

            o_leave(n_blk - 1)

            @pl.loop(0, n_blk)
            def _(i):
                q_v[blk(i), :] = product(i, wx_v[:, 0:q_cols])
                pl.when(i == 0)(lambda: kv_leave(1))

            def more_after_block(i):
                @pl.when(i == 0)
                def _():
                    w_enter(3)

                @pl.when(i == 1)
                def _():
                    w_pass_first(1)
                    w_pass_first(2)

                @pl.when(i == 2)
                def _():
                    w_pass_second(1)
                    w_pass_second(2)

            attention(1, peer_shard(tp, 1), lambda i: None, more_after_block)

    pl.run_scoped(
        attend,
        pltpu.VMEM((chunk, d_model), BF16),
        pltpu.VMEM((2, d_model, 2 * HEAD_DIM), BF16),
        pltpu.VMEM((chunk, q_cols), BF16),
        pltpu.VMEM((chunk, HEAD_DIM), jnp.int32),
        pltpu.VMEM((Q_BLK, chunk), F32),
        pltpu.VMEM((Q_BLK, q_cols), F32),
        pltpu.VMEM((Q_BLK, q_cols), F32),
        pltpu.VMEM((Q_BLK, q_cols), F32),
    )

    def output(acc_v, y_v):
        n_tile = 512

        def multiply(k, c, store):
            shard = tp if k == 0 else peer_shard(tp, k)
            lhs = o_v[shard, piece(c), :]

            @pl.loop(0, n_cols // n_tile)
            def _(n):
                out = pl.ds(pl.multiple_of(n * n_tile, n_tile), n_tile)
                store(out, jnp.dot(lhs, w_v[shard, :, out], preferred_element_type=F32))

        own_w.wait()

        @pl.when(mid == 0)
        def _():
            w_pass_first(3)
            w_pass_second(3)

        @pl.loop(0, n_pc)
        def _(c):
            def store(out, part):
                acc_v[piece(c), out] = part

            multiply(0, c, store)
            pl.when((c == 0) & (mid == 1))(lambda: o_leave(n_blk - 1))

        @pl.when(mid == 1)
        def _():
            for k in (1, 2, 3):
                w_pass_first(k)

            @pl.loop(0, n_pc)
            def _(c):
                o_forward(1, c)
                o_forward(3, c)

            for k in (1, 2, 3):
                w_pass_second(k)

        w_finish(1)

        @pl.loop(0, n_pc)
        def _(c):
            def store(out, part):
                acc_v[piece(c), out] += part

            multiply(1, c, store)

        w_finish(2)

        @pl.loop(0, n_pc)
        def _(c):
            def store(out, part):
                acc_v[piece(c), out] += part

            o_forward(2, c)
            multiply(2, c, store)

        w_finish(3)

        def y_copy(slot, c):
            return pltpu.make_async_copy(y_v.at[slot], y_hbm.at[piece(c)], y_sem.at[slot])

        @pl.loop(0, n_pc)
        def _(c):
            slot = lax.rem(c, 2)
            pl.when(mid == 0)(lambda: o_next(3, c).wait_recv())
            pl.when(c >= 2)(lambda: y_copy(slot, c - 2).wait())

            def store(out, part):
                y_v[slot, :, out] = (acc_v[piece(c), out] + part).astype(BF16)

            multiply(3, c, store)
            y_copy(slot, c).start()

        for c in (n_pc - 2, n_pc - 1):
            y_copy(c % 2, c).wait()

    pl.run_scoped(output, pltpu.VMEM((chunk, n_cols), F32), pltpu.VMEM((2, O_ROWS, n_cols), BF16))

    kv_sent(0)

    @pl.when(mid == 0)
    def _():
        kv_sent(1)
        for hop in range(len(hops)):
            w_copy(4, hop).wait_send()

    pl.when(mid == 1)(lambda: over(wx_copies(), 'wait_send'))
    pl.when(tp < 3)(z_up.wait_send)
    pl.when(tp > 0)(z_down.wait_send)
    for k in (1, 2, 3):
        pl.when(mid == 1)(lambda: z_next(k).wait_send())
        for hop in range(len(hops)):
            w_copy(k, hop).wait_send()

    @pl.loop(0, n_pc)
    def _(c):
        o_own(c).wait_send()

        @pl.when(mid == 1)
        def _():
            for k in (1, 2, 3):
                o_next(k, c).wait_send()


def solution(mesh):
    any_spec = pl.BlockSpec(memory_space=pl.ANY)
    dma = pltpu.SemaphoreType.DMA

    def layer(x_loc, seg_loc, w_query, w_key, w_value, w_out):
        chunk = x_loc.shape[0]
        q_cols = w_query.shape[1]
        n_blk = chunk // Q_BLK
        n_pc = chunk // O_ROWS
        return pl.pallas_call(
            layer_kernel,
            name='layer',
            out_shape=jax.ShapeDtypeStruct((chunk, w_out.shape[1]), BF16),
            in_specs=[any_spec] * 6,
            out_specs=any_spec,
            scratch_shapes=[
                pltpu.VMEM((4,) + w_out.shape, BF16),
                pltpu.VMEM((4, chunk, q_cols), BF16),
                pltpu.VMEM((2, 4 * chunk, 2 * HEAD_DIM), BF16),
                pltpu.VMEM((1, 4 * chunk), jnp.int32),
                pltpu.VMEM((x_loc.shape[1], q_cols + 2 * HEAD_DIM), BF16),
                dma((n_blk + 6,)), dma((2, 3)), dma((2, 3)), dma((3,)), dma((3,)), dma((3,)), dma((3,)), dma((5,)), dma((4,)),
                dma((4, 13)), dma((4, 13)), dma((5, n_pc)), dma((4, n_pc)), dma((2,)),
            ],
            compiler_params=pltpu.CompilerParams(collective_id=0, has_side_effects=True, vmem_limit_bytes=67043328),
        )(x_loc, seg_loc[None, :], w_query, w_key, w_value, w_out)

    return jax.shard_map(layer, mesh=mesh, in_specs=(P(('dp', 'cp'), None), P(('dp', 'cp')), P(None, 'tp'), P(None, 'tp'), P(None, 'tp'), P('tp', None)), out_specs=P(('dp', 'cp'), None), check_vma=False)
```

time: 196 us -> 236 us (1.20)
  the two profiles are of different devices: /device:TPU:0 before, /device:TPU:4 now
where the time goes in v3:
time: 236 us
  Pallas kernels  230 us (97%)
  local copies, waits for them, and re-layouts  6.6 us (3%)
    pallas_call x1, Pallas kernels, layer(): pl.pallas_call(layer_kernel, name='layer', out_shape=jax.ShapeDtypeStruct...  230 us
    unnamed x1, local copies, waits for them, and re-layouts  6.6 us

profile of v3, /device:TPU:4, one launch (start us, length us, event | category | flops | bytes accessed | tf_op | source)
XLA Modules:
  0.0 236.2 jit_solution(5409927431924888929)
XLA Ops:
  0.0 229.5 %layer.1 = bf16[1024,3584]{1,0:T(8,128)(2,1)} custom-call(bf16[1024,3584]{1,0:T(8,128)(2,1)} %x_hbm.1, s32[1,1024]{1,0:T(1,128)} %bitcast.1, bf16[3584,896]{1,0:T(8,128)(2,1)} %wq_hbm.1, bf16[3584,128]{1,0:T(8,128)(2,1)} %wk_hbm.1, bf16[3584,128]{1,0:T(8,128)(2,1)} %wv_hbm.1, bf16[896,3584]{1,0:T(8,128)(2,1)} %wo_hbm.1), custom_call_target="tpu_custom_call" | custom-call | tf_op jit(solution)/shard_map/layer/pallas_call | solution.py:520
  229.6 6.6 %copy.8 = bf16[1024,3584]{1,0:T(8,128)(2,1)} copy(bf16[1024,3584]{1,0:T(8,128)(2,1)} %layer.1) | data formatting | bytes 14680064

commit v4 on v3

--- a/solution.py
+++ b/solution.py
@@ -55,7 +55,7 @@
     heads = q_cols // HEAD_DIM
     n_rows = wo_hbm.shape[0] // 8
     n_cols = wo_hbm.shape[1]
-    half = n_cols // 2
+    part_a = n_cols // HEAD_DIM * 3 // 7 * HEAD_DIM
     x_rows = d_model // 8
     wx_cols = q_cols + 2 * HEAD_DIM
     n_blk = chunk // Q_BLK
@@ -83,18 +83,20 @@
         return z_copy(k, w_v.at[shard, rows_of(dp, cp)], shard, onward(shard))
 
     def x_slice(dp_i, cp_i, part='ab'):
-        first = (dp_i * 4 + cp_i) * x_rows + (x_rows // 2 if part == 'b' else 0)
-        return pl.ds(pl.multiple_of(first, 16), x_rows if part == 'ab' else x_rows // 2)
-
-    def wx_copies():
-        rows = x_slice(dp, cp)
+        rows_a = x_rows * 3 // 7
+        first = (dp_i * 4 + cp_i) * x_rows + (rows_a if part == 'b' else 0)
+        return pl.ds(pl.multiple_of(first, 16), {'a': rows_a, 'b': x_rows - rows_a, 'ab': x_rows}[part])
+
+    def wx_copies(part):
+        rows = x_slice(dp, cp, part)
+        first = 3 * (part == 'b')
         out = []
         for n, (src, lo, hi) in enumerate(((wq_hbm, 0, q_cols), (wk_hbm, q_cols, q_cols + HEAD_DIM), (wv_hbm, q_cols + HEAD_DIM, wx_cols))):
-            out.append(pltpu.make_async_remote_copy(src.at[rows], wx_v.at[rows, lo:hi], x_send.at[n], x_recv.at[n],
+            out.append(pltpu.make_async_remote_copy(src.at[rows], wx_v.at[rows, lo:hi], x_send.at[first + n], x_recv.at[first + n],
                                                     device_id=(dp, tp - 1 + 2 * (tp // 2), cp), device_id_type=MESH))
         return out
 
-    cuts = {'a': pl.ds(0, half), 'b': pl.ds(half, half), 'ab': pl.ds(0, n_cols)}
+    cuts = {'a': pl.ds(0, part_a), 'b': pl.ds(part_a, n_cols - part_a), 'ab': pl.ds(0, n_cols)}
     hops = [('x', 'own', 'a'), ('x', 'own', 'b'), ('x', 'y', 'b'), ('y', 'own', 'b'), ('y', 'own', 'a'), ('y', 'x', 'a'),
             ('c', 'own', 'ab'), ('c', 'x', 'a'), ('c', 'x', 'b'), ('c', 'd', 'b'), ('c', 'y', 'b'), ('c', 'y', 'a'), ('c', 'd', 'a')]
 
@@ -118,39 +120,34 @@
         dp_i, cp_i = {'x': (1 - dp, cp), 'y': (dp, cp_y), 'c': (dp, cp_c)}[hops[hop][0]]
         return w_hop(k, hop, dp_i, cp_i)
 
-    def w_enter(k):
+    def w_arrived(k):
         z_next(k).wait_recv()
         pl.when(mid == 1)(lambda: z_next(k).start())
-        w_spread(k)
-
-    def w_spread(k):
-        for hop in (0, 3, 6, 1, 4):
+
+    def w_send_on(k, *which):
+        for hop in which:
             w_copy(k, hop).start()
 
-    def w_pass_first(k):
-        w_arrival(k, 0).wait_recv()
-        w_copy(k, 5).start()
-        w_copy(k, 7).start()
-        w_arrival(k, 3).wait_recv()
-        w_copy(k, 2).start()
-        w_copy(k, 10).start()
-
-    def w_pass_second(k):
-        w_arrival(k, 1).wait_recv()
-        w_copy(k, 8).start()
-        w_arrival(k, 4).wait_recv()
-        w_copy(k, 11).start()
+    def w_enter(k):
+        w_arrived(k)
+        w_send_on(k, 0, 3, 6, 1, 4)
+
+    def w_relay(k, *which):
+        after = {0: (5, 7), 1: (8,), 2: (9,), 3: (2, 10), 4: (11,), 5: (12,)}
+        for hop in which:
+            w_arrival(k, hop).wait_recv()
+            w_send_on(k, *after[hop])
 
     def w_finish(k):
-        w_arrival(k, 2).wait_recv()
-        w_copy(k, 9).start()
-        w_arrival(k, 5).wait_recv()
-        w_copy(k, 12).start()
+        w_relay(k, 2, 5)
         for hop in range(6, 13):
             w_arrival(k, hop).wait_recv()
 
     def piece(c):
         return pl.ds(pl.multiple_of(c * O_ROWS, O_ROWS), O_ROWS)
+
+    def nth(n):
+        return (n_blk - 1 - n // per_blk) * per_blk + lax.rem(n, per_blk)
 
     def o_copy(slot, c, shard, to):
         at = o_v.at[shard, piece(c)]
@@ -227,7 +224,12 @@
         seg_load.start()
 
         greet(dp, tp, cp, mid)
-        pl.when(mid == 1)(lambda: over(wx_copies(), 'start'))
+
+        @pl.when(mid == 1)
+        def _():
+            over(wx_copies('a'), 'start')
+            over(wx_copies('b'), 'start')
+
         pl.when(tp < 3)(z_up.start)
         pl.when(tp > 0)(z_down.start)
 
@@ -265,15 +267,10 @@
             rows = pl.ds(pl.multiple_of(i * HEAD_DIM, HEAD_DIM), HEAD_DIM)
             col_v[rows, :] = jnp.transpose(jnp.broadcast_to(ids, (HEAD_DIM, HEAD_DIM)))
 
-        @pl.when(mid == 1)
-        def _():
-            w_enter(1)
-            w_enter(3)
-
         @pl.when(mid == 0)
         def _():
-            over(wx_copies(), 'wait_recv')
-            w_spread(4)
+            over(wx_copies('a'), 'wait_recv')
+            w_send_on(4, 0, 4)
 
         def step(g, i, key0, n_keys, first):
             keys = pl.ds(pl.multiple_of(key0, n_keys), n_keys)
@@ -322,72 +319,94 @@
 
         per_loc = LOC_BLK // Q_BLK
 
-        def attention(g, shard, after_first, after_block):
+        def attention(g, shard, after_first, inside, after_block):
             @pl.loop(0, n_blk)
-            def _(i):
+            def _(t):
+                i = n_blk - 1 - t
                 last = i // per_loc
                 step(g, i, cp * chunk + last * LOC_BLK, LOC_BLK, True)
-                after_first(i)
+                after_first(t)
 
                 @pl.loop(0, last)
                 def _(j):
                     step(g, i, cp * chunk + j * LOC_BLK, LOC_BLK, False)
 
-                pl.when(i == 0)(lambda: kv_wait(g))
+                pl.when(t == 0)(lambda: kv_wait(g))
 
                 @pl.loop(0, cp)
                 def _(j):
                     step(g, i, j * chunk, chunk, False)
-
+                    if inside is not None:
+                        pl.when((t == 0) & (j == 0))(inside)
+
+                if inside is not None:
+                    pl.when((t == 0) & (cp == 0))(inside)
                 for h in range(heads):
                     cols = slice(h * HEAD_DIM, (h + 1) * HEAD_DIM)
                     total = jnp.sum(l_v[:, cols], axis=1, keepdims=True)
                     o_v[shard, blk(i), cols] = (acc_v[:, cols] / total).astype(BF16)
-                after_block(i)
-
-        def own_after_first(i):
-            pl.when(i > 0)(lambda: o_leave(i - 1))
-
-        def own_after_block(i):
-            pl.when((i == 0) & (mid == 1))(lambda: w_enter(2))
-            pl.when((i == 0) & (mid == 0))(lambda: w_pass_first(4))
-            pl.when((i == 1) & (mid == 0))(lambda: w_enter(1))
-            pl.when((i == 2) & (mid == 0))(lambda: w_pass_second(4))
-
-        attention(0, tp, own_after_first, own_after_block)
+                after_block(t)
+
+        def own_after_first(t):
+            pl.when(t > 0)(lambda: o_leave(n_blk - t))
+
+        def own_inside():
+            @pl.when(mid == 1)
+            def _():
+                w_enter(1)
+                w_enter(3)
+
+            @pl.when(mid == 0)
+            def _():
+                over(wx_copies('b'), 'wait_recv')
+                w_send_on(4, 3, 1, 6)
+
+        def own_after_block(t):
+            pl.when((t == 1) & (mid == 1))(lambda: w_enter(2))
+            pl.when((t == 0) & (mid == 0))(lambda: w_relay(4, 0, 4))
+
+            @pl.when((t == 1) & (mid == 0))
+            def _():
+                w_relay(4, 3, 1)
+                w_arrived(1)
+                w_send_on(1, 0, 3, 6, 1)
+
+        attention(0, tp, own_after_first, own_inside, own_after_block)
 
         @pl.when(mid == 0)
         def _():
             w_finish(4)
-            w_enter(2)
 
             @pl.loop(0, n_blk)
             def _(i):
                 kv_v[1, own_rows(i), :] = product(i, wx_v[:, q_cols:wx_cols])
 
-            o_leave(n_blk - 1)
+            o_leave(0)
 
             @pl.loop(0, n_blk)
             def _(i):
                 q_v[blk(i), :] = product(i, wx_v[:, 0:q_cols])
-                pl.when(i == 0)(lambda: kv_leave(1))
-
-            def more_after_block(i):
+
                 @pl.when(i == 0)
                 def _():
+                    kv_leave(1)
+                    w_send_on(1, 4)
+                    w_enter(2)
+
+            def more_after_block(t):
+                @pl.when(t == 0)
+                def _():
+                    w_relay(1, 0, 3)
                     w_enter(3)
 
-                @pl.when(i == 1)
+                @pl.when(t == 1)
                 def _():
-                    w_pass_first(1)
-                    w_pass_first(2)
-
-                @pl.when(i == 2)
-                def _():
-                    w_pass_second(1)
-                    w_pass_second(2)
-
-            attention(1, peer_shard(tp, 1), lambda i: None, more_after_block)
+                    w_relay(1, 1, 4)
+                    w_relay(2, 0, 3)
+
+                pl.when(t == 2)(lambda: w_relay(2, 1, 4))
+
+            attention(1, peer_shard(tp, 1), lambda t: None, None, more_after_block)
 
     pl.run_scoped(
         attend,
@@ -404,83 +423,97 @@
     def output(acc_v, y_v):
         n_tile = 512
 
-        def multiply(k, c, store):
-            shard = tp if k == 0 else peer_shard(tp, k)
-            lhs = o_v[shard, piece(c), :]
-
+        big = 2 * Q_BLK
+
+        def multiply(ks, rows, store):
             @pl.loop(0, n_cols // n_tile)
             def _(n):
                 out = pl.ds(pl.multiple_of(n * n_tile, n_tile), n_tile)
-                store(out, jnp.dot(lhs, w_v[shard, :, out], preferred_element_type=F32))
+                parts = []
+                for k in ks:
+                    shard = tp if k == 0 else peer_shard(tp, k)
+                    parts.append(jnp.dot(o_v[shard, rows, :], w_v[shard, :, out], preferred_element_type=F32))
+                store(out, functools.reduce(jnp.add, parts))
+
+        def span(i, size):
+            return pl.ds(pl.multiple_of(i * size, size), size)
 
         own_w.wait()
 
+        @pl.when(mid == 1)
+        def _():
+            w_relay(1, 0, 3)
+            o_leave(0)
+            w_relay(3, 0, 3)
+            w_relay(1, 1, 4)
+            w_relay(3, 1, 4)
+
+            @pl.loop(0, n_pc)
+            def _(n):
+                o_forward(1, nth(n))
+                o_forward(3, nth(n))
+
+            w_relay(2, 0, 3, 1, 4)
+
         @pl.when(mid == 0)
         def _():
-            w_pass_first(3)
-            w_pass_second(3)
-
-        @pl.loop(0, n_pc)
-        def _(c):
+            w_relay(3, 0, 3)
+
+        w_finish(1)
+
+        @pl.loop(0, chunk // big)
+        def _(i):
+            rows = span(i, big)
+
             def store(out, part):
-                acc_v[piece(c), out] = part
-
-            multiply(0, c, store)
-            pl.when((c == 0) & (mid == 1))(lambda: o_leave(n_blk - 1))
-
-        @pl.when(mid == 1)
-        def _():
-            for k in (1, 2, 3):
-                w_pass_first(k)
-
-            @pl.loop(0, n_pc)
-            def _(c):
-                o_forward(1, c)
-                o_forward(3, c)
-
-            for k in (1, 2, 3):
-                w_pass_second(k)
-
-        w_finish(1)
-
-        @pl.loop(0, n_pc)
-        def _(c):
+                acc_v[rows, out] = part
+
+            multiply((0, 1), rows, store)
+
+        pl.when(mid == 0)(lambda: w_relay(3, 1, 4))
+        w_finish(2)
+
+        @pl.loop(0, chunk // big)
+        def _(n):
+            for j in range(big // O_ROWS):
+                o_forward(2, nth(n * (big // O_ROWS) + j))
+            rows = span(chunk // big - 1 - n, big)
+
             def store(out, part):
-                acc_v[piece(c), out] += part
-
-            multiply(1, c, store)
-
-        w_finish(2)
-
-        @pl.loop(0, n_pc)
-        def _(c):
+                acc_v[rows, out] += part
+
+            multiply((2,), rows, store)
+
+        w_finish(3)
+
+        def last_shard(first, pieces, slot):
+            n_out = pieces * O_ROWS
+            row0 = chunk - (first + pieces) * O_ROWS if pieces > 1 else (first - (n_pc - per_blk)) * O_ROWS
+            rows = pl.ds(row0, n_out)
+
+            @pl.when(mid == 0)
+            def _():
+                for n in range(first, first + pieces):
+                    o_next(3, nth(n)).wait_recv()
+
+            held = pl.ds(first * O_ROWS if pieces > 1 else row0, n_out)
+
             def store(out, part):
-                acc_v[piece(c), out] += part
-
-            o_forward(2, c)
-            multiply(2, c, store)
-
-        w_finish(3)
-
-        def y_copy(slot, c):
-            return pltpu.make_async_copy(y_v.at[slot], y_hbm.at[piece(c)], y_sem.at[slot])
-
-        @pl.loop(0, n_pc)
-        def _(c):
-            slot = lax.rem(c, 2)
-            pl.when(mid == 0)(lambda: o_next(3, c).wait_recv())
-            pl.when(c >= 2)(lambda: y_copy(slot, c - 2).wait())
-
-            def store(out, part):
-                y_v[slot, :, out] = (acc_v[piece(c), out] + part).astype(BF16)
-
-            multiply(3, c, store)
-            y_copy(slot, c).start()
-
-        for c in (n_pc - 2, n_pc - 1):
-            y_copy(c % 2, c).wait()
-
-    pl.run_scoped(output, pltpu.VMEM((chunk, n_cols), F32), pltpu.VMEM((2, O_ROWS, n_cols), BF16))
+                y_v[held, out] = (acc_v[rows, out] + part).astype(BF16)
+
+            multiply((3,), rows, store)
+            copy = pltpu.make_async_copy(y_v.at[held], y_hbm.at[rows], y_sem.at[slot])
+            copy.start()
+            return copy
+
+        copies = [last_shard(0, n_pc // 2, 0), last_shard(n_pc // 2, per_blk, 1)]
+        copies[0].wait()
+        for n in range(n_pc - per_blk, n_pc):
+            copies.append(last_shard(n, 1, len(copies)))
+        for copy in copies[1:]:
+            copy.wait()
+
+    pl.run_scoped(output, pltpu.VMEM((chunk, n_cols), F32), pltpu.VMEM((chunk - Q_BLK, n_cols), BF16))
 
     kv_sent(0)
 
@@ -490,7 +523,11 @@
         for hop in range(len(hops)):
             w_copy(4, hop).wait_send()
 
-    pl.when(mid == 1)(lambda: over(wx_copies(), 'wait_send'))
+    @pl.when(mid == 1)
+    def _():
+        over(wx_copies('a'), 'wait_send')
+        over(wx_copies('b'), 'wait_send')
+
     pl.when(tp < 3)(z_up.wait_send)
     pl.when(tp > 0)(z_down.wait_send)
     for k in (1, 2, 3):
@@ -529,8 +566,8 @@
                 pltpu.VMEM((2, 4 * chunk, 2 * HEAD_DIM), BF16),
                 pltpu.VMEM((1, 4 * chunk), jnp.int32),
                 pltpu.VMEM((x_loc.shape[1], q_cols + 2 * HEAD_DIM), BF16),
-                dma((n_blk + 6,)), dma((2, 3)), dma((2, 3)), dma((3,)), dma((3,)), dma((3,)), dma((3,)), dma((5,)), dma((4,)),
-                dma((4, 13)), dma((4, 13)), dma((5, n_pc)), dma((4, n_pc)), dma((2,)),
+                dma((n_blk + 6,)), dma((2, 3)), dma((2, 3)), dma((3,)), dma((3,)), dma((6,)), dma((6,)), dma((5,)), dma((4,)),
+                dma((4, 13)), dma((4, 13)), dma((5, n_pc)), dma((4, n_pc)), dma((4,)),
             ],
             compiler_params=pltpu.CompilerParams(collective_id=0, has_side_effects=True, vmem_limit_bytes=67043328),
         )(x_loc, seg_loc[None, :], w_query, w_key, w_value, w_out)

time: 236 us -> 179 us (0.76)
  the two profiles are of different devices: /device:TPU:4 before, /device:TPU:28 now
where the time goes in v4:
time: 179 us; the launch traced here: 178 us
  Pallas kernels  172 us (96%)
  local copies, waits for them, and re-layouts  6.6 us (4%)
    pallas_call x1, Pallas kernels, layer(): pl.pallas_call(layer_kernel, name='layer', out_shape=jax.ShapeDtypeStruct...  172 us
    unnamed x1, local copies, waits for them, and re-layouts  6.6 us

profile of v4, /device:TPU:28, one launch (start us, length us, event | category | flops | bytes accessed | tf_op | source)
XLA Modules:
  0.0 178.4 jit_solution(8066206318946727216)
XLA Ops:
  0.0 171.8 %layer.1 = bf16[1024,3584]{1,0:T(8,128)(2,1)} custom-call(bf16[1024,3584]{1,0:T(8,128)(2,1)} %x_hbm.1, s32[1,1024]{1,0:T(1,128)} %bitcast.1, bf16[3584,896]{1,0:T(8,128)(2,1)} %wq_hbm.1, bf16[3584,128]{1,0:T(8,128)(2,1)} %wk_hbm.1, bf16[3584,128]{1,0:T(8,128)(2,1)} %wv_hbm.1, bf16[896,3584]{1,0:T(8,128)(2,1)} %wo_hbm.1), custom_call_target="tpu_custom_call" | custom-call | tf_op jit(solution)/shard_map/layer/pallas_call | solution.py:557
  171.8 6.6 %copy.8 = bf16[1024,3584]{1,0:T(8,128)(2,1)} copy(bf16[1024,3584]{1,0:T(8,128)(2,1)} %layer.1) | data formatting | bytes 14680064

commit v5 on v4

--- a/solution.py
+++ b/solution.py
@@ -40,8 +40,8 @@
     if k == 1:
         return tp + 1 - 2 * lax.rem(tp, 2)
     if k == 2:
-        return lax.rem(tp + 2, 4)
-    return 3 - tp
+        return 2 - tp // 2
+    return 3 * (1 - tp // 2)
 
 
 def layer_kernel(x_hbm, seg_hbm, wq_hbm, wk_hbm, wv_hbm, wo_hbm, y_hbm,
@@ -139,7 +139,6 @@
             w_send_on(k, *after[hop])
 
     def w_finish(k):
-        w_relay(k, 2, 5)
         for hop in range(6, 13):
             w_arrival(k, hop).wait_recv()
 
@@ -243,9 +242,12 @@
             return jnp.dot(x_v[blk(i), :], w, preferred_element_type=F32).astype(BF16)
 
         over(w_loads[0], 'wait')
-        for i in range(n_blk):
-            x_loads[i].wait()
+
+        @pl.loop(0, n_blk)
+        def _(i):
+            pltpu.make_async_copy(x_hbm.at[blk(i)], x_v.at[blk(i)], load_sem.at[i]).wait()
             kv_v[0, own_rows(i), :] = product(i, w_blk[0])
+
         over(w_loads[2], 'start')
         seg_load.wait()
         for n, (lo, hi) in enumerate(spans):
@@ -254,11 +256,11 @@
             @pl.loop(0, n_blk)
             def _(i):
                 q_v[blk(i), lo:hi] = product(i, w_blk[(n + 1) % 2, :, 0:hi - lo])
+                if n == 0:
+                    pl.when(i == 0)(lambda: kv_leave(0))
 
             if n + 3 < len(w_loads):
                 over(w_loads[n + 3], 'start')
-            if n == 0:
-                kv_leave(0)
         own_w.start()
 
         @pl.loop(0, chunk // HEAD_DIM)
@@ -349,12 +351,13 @@
 
         def own_after_first(t):
             pl.when(t > 0)(lambda: o_leave(n_blk - t))
+            pl.when((t == 3) & (mid == 0))(lambda: w_relay(4, 2, 5))
 
         def own_inside():
             @pl.when(mid == 1)
             def _():
                 w_enter(1)
-                w_enter(3)
+                w_enter(2)
 
             @pl.when(mid == 0)
             def _():
@@ -362,14 +365,14 @@
                 w_send_on(4, 3, 1, 6)
 
         def own_after_block(t):
-            pl.when((t == 1) & (mid == 1))(lambda: w_enter(2))
+            pl.when((t == 1) & (mid == 1))(lambda: w_enter(3))
             pl.when((t == 0) & (mid == 0))(lambda: w_relay(4, 0, 4))
 
             @pl.when((t == 1) & (mid == 0))
             def _():
                 w_relay(4, 3, 1)
                 w_arrived(1)
-                w_send_on(1, 0, 3, 6, 1)
+                w_send_on(1, 0, 3, 6, 1, 4)
 
         attention(0, tp, own_after_first, own_inside, own_after_block)
 
@@ -390,23 +393,22 @@
                 @pl.when(i == 0)
                 def _():
                     kv_leave(1)
-                    w_send_on(1, 4)
+                    w_relay(1, 0, 3)
                     w_enter(2)
+
+            def more_after_first(t):
+                pl.when(t == 2)(lambda: w_relay(1, 2, 5))
 
             def more_after_block(t):
                 @pl.when(t == 0)
                 def _():
-                    w_relay(1, 0, 3)
+                    w_relay(1, 1, 4)
                     w_enter(3)
 
-                @pl.when(t == 1)
-                def _():
-                    w_relay(1, 1, 4)
-                    w_relay(2, 0, 3)
-
+                pl.when(t == 1)(lambda: w_relay(2, 0, 3))
                 pl.when(t == 2)(lambda: w_relay(2, 1, 4))
 
-            attention(1, peer_shard(tp, 1), lambda t: None, None, more_after_block)
+            attention(1, peer_shard(tp, 1), more_after_first, None, more_after_block)
 
     pl.run_scoped(
         attend,
@@ -421,22 +423,19 @@
     )
 
     def output(acc_v, y_v):
-        n_tile = 512
-
-        big = 2 * Q_BLK
-
-        def multiply(ks, rows, store):
-            @pl.loop(0, n_cols // n_tile)
+        n_tile = 256
+
+        def multiply(ks, rows, width, store, between):
+            @pl.loop(0, n_cols // width)
             def _(n):
-                out = pl.ds(pl.multiple_of(n * n_tile, n_tile), n_tile)
+                out = pl.ds(pl.multiple_of(n * width, width), width)
                 parts = []
                 for k in ks:
                     shard = tp if k == 0 else peer_shard(tp, k)
                     parts.append(jnp.dot(o_v[shard, rows, :], w_v[shard, :, out], preferred_element_type=F32))
                 store(out, functools.reduce(jnp.add, parts))
-
-        def span(i, size):
-            return pl.ds(pl.multiple_of(i * size, size), size)
+                if between is not None:
+                    between(n)
 
         own_w.wait()
 
@@ -444,47 +443,56 @@
         def _():
             w_relay(1, 0, 3)
             o_leave(0)
-            w_relay(3, 0, 3)
+            w_relay(2, 0, 3)
             w_relay(1, 1, 4)
-            w_relay(3, 1, 4)
+            w_relay(2, 1, 4)
 
             @pl.loop(0, n_pc)
             def _(n):
                 o_forward(1, nth(n))
+                o_forward(2, nth(n))
+
+            w_relay(3, 0, 3, 1, 4)
+            w_relay(1, 2, 5)
+
+        pl.when(mid == 0)(lambda: w_relay(3, 0))
+        w_finish(1)
+
+        def during_first(n):
+            pl.when((n == 4) & (mid == 0))(lambda: w_relay(3, 3))
+
+            @pl.when(n == 8)
+            def _():
+                w_relay(2, 2, 5)
+                pl.when(mid == 0)(lambda: w_relay(3, 1))
+
+            pl.when((n == 11) & (mid == 0))(lambda: w_relay(3, 4))
+
+        def during_second(n):
+            pl.when(n == 9)(lambda: w_relay(3, 2, 5))
+
+        def begin(out, part):
+            acc_v[:, out] = part
+
+        def add(out, part):
+            acc_v[:, out] += part
+
+        multiply((0, 1), slice(None), n_tile, begin, during_first)
+        w_finish(2)
+
+        @pl.loop(0, n_pc)
+        def _(n):
+            pl.when(mid == 0)(lambda: o_next(2, nth(n)).wait_recv())
+            pl.when((mid == 1) & (n < n_pc // 2))(lambda: o_forward(3, nth(n)))
+
+        multiply((2,), slice(None), n_tile, add, during_second)
+        w_finish(3)
+
+        @pl.when(mid == 1)
+        def _():
+            @pl.loop(n_pc // 2, n_pc)
+            def _(n):
                 o_forward(3, nth(n))
-
-            w_relay(2, 0, 3, 1, 4)
-
-        @pl.when(mid == 0)
-        def _():
-            w_relay(3, 0, 3)
-
-        w_finish(1)
-
-        @pl.loop(0, chunk // big)
-        def _(i):
-            rows = span(i, big)
-
-            def store(out, part):
-                acc_v[rows, out] = part
-
-            multiply((0, 1), rows, store)
-
-        pl.when(mid == 0)(lambda: w_relay(3, 1, 4))
-        w_finish(2)
-
-        @pl.loop(0, chunk // big)
-        def _(n):
-            for j in range(big // O_ROWS):
-                o_forward(2, nth(n * (big // O_ROWS) + j))
-            rows = span(chunk // big - 1 - n, big)
-
-            def store(out, part):
-                acc_v[rows, out] += part
-
-            multiply((2,), rows, store)
-
-        w_finish(3)
 
         def last_shard(first, pieces, slot):
             n_out = pieces * O_ROWS
@@ -501,7 +509,7 @@
             def store(out, part):
                 y_v[held, out] = (acc_v[rows, out] + part).astype(BF16)
 
-            multiply((3,), rows, store)
+            multiply((3,), rows, 2 * n_tile, store, None)
             copy = pltpu.make_async_copy(y_v.at[held], y_hbm.at[rows], y_sem.at[slot])
             copy.start()
             return copy

time: 179 us -> 171 us (0.955)
  the two profiles are of different devices: /device:TPU:28 before, /device:TPU:0 now
where the time goes in v5:
time: 171 us; the launch traced here: 169 us
  Pallas kernels  163 us (95%)
  local copies, waits for them, and re-layouts  6.6 us (4%)
    pallas_call x1, Pallas kernels, layer(): pl.pallas_call(layer_kernel, name='layer', out_shape=jax.ShapeDtypeStruct...  163 us
    unnamed x1, local copies, waits for them, and re-layouts  6.6 us

profile of v5, /device:TPU:0, one launch (start us, length us, event | category | flops | bytes accessed | tf_op | source)
XLA Modules:
  0.0 169.4 jit_solution(6512410958015768200)
XLA Ops:
  0.0 162.8 %layer.1 = bf16[1024,3584]{1,0:T(8,128)(2,1)} custom-call(bf16[1024,3584]{1,0:T(8,128)(2,1)} %x_hbm.1, s32[1,1024]{1,0:T(1,128)} %bitcast.1, bf16[3584,896]{1,0:T(8,128)(2,1)} %wq_hbm.1, bf16[3584,128]{1,0:T(8,128)(2,1)} %wk_hbm.1, bf16[3584,128]{1,0:T(8,128)(2,1)} %wv_hbm.1, bf16[896,3584]{1,0:T(8,128)(2,1)} %wo_hbm.1), custom_call_target="tpu_custom_call" | custom-call | tf_op jit(solution)/shard_map/layer/pallas_call | solution.py:565
  162.8 6.6 %copy.8 = bf16[1024,3584]{1,0:T(8,128)(2,1)} copy(bf16[1024,3584]{1,0:T(8,128)(2,1)} %layer.1) | data formatting | bytes 14680064

commit v6 on v5

--- a/solution.py
+++ b/solution.py
@@ -44,9 +44,9 @@
     return 3 * (1 - tp // 2)
 
 
-def layer_kernel(x_hbm, seg_hbm, wq_hbm, wk_hbm, wv_hbm, wo_hbm, y_hbm,
-                 w_v, o_v, kv_v, seg_v, wx_v,
-                 load_sem, kv_send, kv_recv, seg_send, seg_recv, x_send, x_recv, z_send, z_recv, w_send, w_recv, o_send, o_recv, y_sem):
+def layer_kernel(x_hbm, seg_hbm, wq_hbm, wk_hbm, wv_hbm, wo_hbm, y_ref,
+                 w_v, o_v, kv_v, seg_v,
+                 load_sem, kv_send, kv_recv, seg_send, seg_recv, x_send, x_recv, z_send, z_recv, w_send, w_recv, o_send, o_recv):
     dp, tp, cp = coords()
     mid = lax.rem((tp + 1) // 2, 2)
     core = lax.rem(cp, 2)
@@ -87,7 +87,7 @@
         first = (dp_i * 4 + cp_i) * x_rows + (rows_a if part == 'b' else 0)
         return pl.ds(pl.multiple_of(first, 16), {'a': rows_a, 'b': x_rows - rows_a, 'ab': x_rows}[part])
 
-    def wx_copies(part):
+    def wx_copies(wx_v, part):
         rows = x_slice(dp, cp, part)
         first = 3 * (part == 'b')
         out = []
@@ -104,10 +104,12 @@
         far = lax.rem(cp_i + 2, 4)
         return {'own': (dp_i, cp_i), 'x': (1 - dp_i, cp_i), 'y': (dp_i, far), 'd': (1 - dp_i, far)}[name]
 
+    wx = []
+
     def w_hop(k, hop, dp_i, cp_i):
         route, name, part = hops[hop]
         if k == 4:
-            at = wx_v.at[x_slice(*holder(name, dp_i, cp_i), part)]
+            at = wx[0].at[x_slice(*holder(name, dp_i, cp_i), part)]
         else:
             at = w_v.at[peer_shard(tp, k), rows_of(*holder(name, dp_i, cp_i)), cuts[part]]
         dev = {'x': dev_x, 'y': dev_y, 'c': dev_c}[route]
@@ -203,7 +205,9 @@
 
     own_w = pltpu.make_async_copy(wo_hbm, w_v.at[tp], load_sem.at[n_blk + 5])
 
-    def attend(x_v, w_blk, q_v, col_v, bias_v, m_v, l_v, acc_v):
+    def attend(wx_v, w_blk, q_v, col_v, bias_v, m_v, l_v, acc_v):
+        wx.append(wx_v)
+        x_v = y_ref
         n_w = 2 * HEAD_DIM
         own = pl.ds(pl.multiple_of(cp * chunk, chunk), chunk)
         x_loads = []
@@ -226,8 +230,8 @@
 
         @pl.when(mid == 1)
         def _():
-            over(wx_copies('a'), 'start')
-            over(wx_copies('b'), 'start')
+            over(wx_copies(wx_v, 'a'), 'start')
+            over(wx_copies(wx_v, 'b'), 'start')
 
         pl.when(tp < 3)(z_up.start)
         pl.when(tp > 0)(z_down.start)
@@ -271,7 +275,7 @@
 
         @pl.when(mid == 0)
         def _():
-            over(wx_copies('a'), 'wait_recv')
+            over(wx_copies(wx_v, 'a'), 'wait_recv')
             w_send_on(4, 0, 4)
 
         def step(g, i, key0, n_keys, first):
@@ -361,7 +365,7 @@
 
             @pl.when(mid == 0)
             def _():
-                over(wx_copies('b'), 'wait_recv')
+                over(wx_copies(wx_v, 'b'), 'wait_recv')
                 w_send_on(4, 3, 1, 6)
 
         def own_after_block(t):
@@ -409,10 +413,17 @@
                 pl.when(t == 2)(lambda: w_relay(2, 1, 4))
 
             attention(1, peer_shard(tp, 1), more_after_first, None, more_after_block)
+            for hop in range(len(hops)):
+                w_copy(4, hop).wait_send()
+
+        @pl.when(mid == 1)
+        def _():
+            over(wx_copies(wx_v, 'a'), 'wait_send')
+            over(wx_copies(wx_v, 'b'), 'wait_send')
 
     pl.run_scoped(
         attend,
-        pltpu.VMEM((chunk, d_model), BF16),
+        pltpu.VMEM((d_model, wx_cols), BF16),
         pltpu.VMEM((2, d_model, 2 * HEAD_DIM), BF16),
         pltpu.VMEM((chunk, q_cols), BF16),
         pltpu.VMEM((chunk, HEAD_DIM), jnp.int32),
@@ -422,7 +433,7 @@
         pltpu.VMEM((Q_BLK, q_cols), F32),
     )
 
-    def output(acc_v, y_v):
+    def output(acc_v):
         n_tile = 256
 
         def multiply(ks, rows, width, store, between):
@@ -494,48 +505,30 @@
             def _(n):
                 o_forward(3, nth(n))
 
-        def last_shard(first, pieces, slot):
-            n_out = pieces * O_ROWS
+        def last_shard(first, pieces):
             row0 = chunk - (first + pieces) * O_ROWS if pieces > 1 else (first - (n_pc - per_blk)) * O_ROWS
-            rows = pl.ds(row0, n_out)
+            rows = pl.ds(row0, pieces * O_ROWS)
 
             @pl.when(mid == 0)
             def _():
                 for n in range(first, first + pieces):
                     o_next(3, nth(n)).wait_recv()
 
-            held = pl.ds(first * O_ROWS if pieces > 1 else row0, n_out)
-
             def store(out, part):
-                y_v[held, out] = (acc_v[rows, out] + part).astype(BF16)
+                y_ref[rows, out] = (acc_v[rows, out] + part).astype(BF16)
 
             multiply((3,), rows, 2 * n_tile, store, None)
-            copy = pltpu.make_async_copy(y_v.at[held], y_hbm.at[rows], y_sem.at[slot])
-            copy.start()
-            return copy
-
-        copies = [last_shard(0, n_pc // 2, 0), last_shard(n_pc // 2, per_blk, 1)]
-        copies[0].wait()
+
+        last_shard(0, n_pc // 2)
+        last_shard(n_pc // 2, per_blk)
         for n in range(n_pc - per_blk, n_pc):
-            copies.append(last_shard(n, 1, len(copies)))
-        for copy in copies[1:]:
-            copy.wait()
-
-    pl.run_scoped(output, pltpu.VMEM((chunk, n_cols), F32), pltpu.VMEM((chunk - Q_BLK, n_cols), BF16))
+            last_shard(n, 1)
+
+    pl.run_scoped(output, pltpu.VMEM((chunk, n_cols), F32))
 
     kv_sent(0)
 
-    @pl.when(mid == 0)
-    def _():
-        kv_sent(1)
-        for hop in range(len(hops)):
-            w_copy(4, hop).wait_send()
-
-    @pl.when(mid == 1)
-    def _():
-        over(wx_copies('a'), 'wait_send')
-        over(wx_copies('b'), 'wait_send')
-
+    pl.when(mid == 0)(lambda: kv_sent(1))
     pl.when(tp < 3)(z_up.wait_send)
     pl.when(tp > 0)(z_down.wait_send)
     for k in (1, 2, 3):
@@ -565,19 +558,18 @@
         return pl.pallas_call(
             layer_kernel,
             name='layer',
-            out_shape=jax.ShapeDtypeStruct((chunk, w_out.shape[1]), BF16),
+            out_shape=pltpu.VMEM((chunk, w_out.shape[1]), BF16),
             in_specs=[any_spec] * 6,
-            out_specs=any_spec,
+            out_specs=pl.BlockSpec(memory_space=pltpu.VMEM),
             scratch_shapes=[
                 pltpu.VMEM((4,) + w_out.shape, BF16),
                 pltpu.VMEM((4, chunk, q_cols), BF16),
                 pltpu.VMEM((2, 4 * chunk, 2 * HEAD_DIM), BF16),
                 pltpu.VMEM((1, 4 * chunk), jnp.int32),
-                pltpu.VMEM((x_loc.shape[1], q_cols + 2 * HEAD_DIM), BF16),
                 dma((n_blk + 6,)), dma((2, 3)), dma((2, 3)), dma((3,)), dma((3,)), dma((6,)), dma((6,)), dma((5,)), dma((4,)),
-                dma((4, 13)), dma((4, 13)), dma((5, n_pc)), dma((4, n_pc)), dma((4,)),
+                dma((4, 13)), dma((4, 13)), dma((5, n_pc)), dma((4, n_pc)),
             ],
-            compiler_params=pltpu.CompilerParams(collective_id=0, has_side_effects=True, vmem_limit_bytes=67043328),
+            compiler_params=pltpu.CompilerParams(collective_id=0, has_side_effects=True, vmem_limit_bytes=59600000),
         )(x_loc, seg_loc[None, :], w_query, w_key, w_value, w_out)
 
     return jax.shard_map(layer, mesh=mesh, in_specs=(P(('dp', 'cp'), None), P(('dp', 'cp')), P(None, 'tp'), P(None, 'tp'), P(None, 'tp'), P('tp', None)), out_specs=P(('dp', 'cp'), None), check_vma=False)

time: 171 us -> 166 us (0.971)
  local copies, waits for them, and re-layouts: 6.6 us -> 3.05 us
    unnamed x1, local copies, waits for them, and re-layouts: 6.6 us -> 3.05 us
where the time goes in v6:
time: 166 us; the launch traced here: 165 us
  Pallas kernels  162 us (98%)
  local copies, waits for them, and re-layouts  3.05 us (2%)
    pallas_call x1, Pallas kernels, layer(): pl.pallas_call(layer_kernel, name='layer', out_shape=pltpu.VMEM((chunk, w...  162 us

profile of v6, /device:TPU:0, one launch (start us, length us, event | category | flops | bytes accessed | tf_op | source)
XLA Modules:
  0.0 164.9 jit_solution(1329424981344573527)
XLA Ops:
  0.0 161.8 %layer.1 = bf16[1024,3584]{1,0:T(8,128)(2,1)S(1)} custom-call(bf16[1024,3584]{1,0:T(8,128)(2,1)} %x_hbm.1, s32[1,1024]{1,0:T(1,128)} %bitcast.1, bf16[3584,896]{1,0:T(8,128)(2,1)} %wq_hbm.1, bf16[3584,128]{1,0:T(8,128)(2,1)} %wk_hbm.1, bf16[3584,128]{1,0:T(8,128)(2,1)} %wv_hbm.1, bf16[896,3584]{1,0:T(8,128)(2,1)} %wo_hbm.1), custom_call_target="tpu_custom_call" | custom-call | tf_op jit(solution)/shard_map/layer/pallas_call | solution.py:558
  161.8 3.1 %copy.8 = bf16[1024,3584]{1,0:T(8,128)(2,1)} copy(bf16[1024,3584]{1,0:T(8,128)(2,1)S(1)} %layer.1) | data formatting | bytes 14680064

commit v7 on v6

--- a/solution.py
+++ b/solution.py
@@ -113,7 +113,7 @@
         else:
             at = w_v.at[peer_shard(tp, k), rows_of(*holder(name, dp_i, cp_i)), cuts[part]]
         dev = {'x': dev_x, 'y': dev_y, 'c': dev_c}[route]
-        return pltpu.make_async_remote_copy(at, at, w_send.at[k - 1, hop], w_recv.at[k - 1, hop], device_id=dev, device_id_type=MESH)
+        return pltpu.make_async_remote_copy(at, at, w_send.at[k - 1], w_recv.at[k - 1, min(hop, 6)], device_id=dev, device_id_type=MESH)
 
     def w_copy(k, hop):
         return w_hop(k, hop, dp, cp)
@@ -140,9 +140,12 @@
             w_arrival(k, hop).wait_recv()
             w_send_on(k, *after[hop])
 
+    def w_bulk(k, slices):
+        at = wx[0].at[0:slices * x_rows] if k == 4 else w_v.at[peer_shard(tp, k), 0:slices * n_rows]
+        return pltpu.make_async_remote_copy(at, at, w_send.at[k - 1], w_recv.at[k - 1, 6], device_id=dev_c, device_id_type=MESH)
+
     def w_finish(k):
-        for hop in range(6, 13):
-            w_arrival(k, hop).wait_recv()
+        w_bulk(k, 4).wait_recv()
 
     def piece(c):
         return pl.ds(pl.multiple_of(c * O_ROWS, O_ROWS), O_ROWS)
@@ -152,7 +155,7 @@
 
     def o_copy(slot, c, shard, to):
         at = o_v.at[shard, piece(c)]
-        return pltpu.make_async_remote_copy(at, at, o_send.at[slot, c], o_recv.at[shard, c], device_id=(dp, to, cp), device_id_type=MESH)
+        return pltpu.make_async_remote_copy(at, at, o_send.at[slot], o_recv.at[shard, c], device_id=(dp, to, cp), device_id_type=MESH)
 
     def o_own(c):
         return o_copy(0, c, tp, tp + 1 - 2 * (tp // 2))
@@ -330,7 +333,9 @@
             def _(t):
                 i = n_blk - 1 - t
                 last = i // per_loc
-                step(g, i, cp * chunk + last * LOC_BLK, LOC_BLK, True)
+                odd = lax.rem(i, per_loc)
+                pl.when(odd == 1)(lambda: step(g, i, cp * chunk + last * LOC_BLK, LOC_BLK, True))
+                pl.when(odd == 0)(lambda: step(g, i, cp * chunk + i * Q_BLK, Q_BLK, True))
                 after_first(t)
 
                 @pl.loop(0, last)
@@ -413,8 +418,7 @@
                 pl.when(t == 2)(lambda: w_relay(2, 1, 4))
 
             attention(1, peer_shard(tp, 1), more_after_first, None, more_after_block)
-            for hop in range(len(hops)):
-                w_copy(4, hop).wait_send()
+            w_bulk(4, 7).wait_send()
 
         @pl.when(mid == 1)
         def _():
@@ -533,17 +537,18 @@
     pl.when(tp > 0)(z_down.wait_send)
     for k in (1, 2, 3):
         pl.when(mid == 1)(lambda: z_next(k).wait_send())
-        for hop in range(len(hops)):
-            w_copy(k, hop).wait_send()
-
-    @pl.loop(0, n_pc)
-    def _(c):
-        o_own(c).wait_send()
-
-        @pl.when(mid == 1)
-        def _():
-            for k in (1, 2, 3):
-                o_next(k, c).wait_send()
+        w_bulk(k, 7).wait_send()
+
+    def o_sent(slot, shard):
+        at = o_v.at[shard]
+        pltpu.make_async_remote_copy(at, at, o_send.at[slot], o_recv.at[shard, 0], device_id=dev_c, device_id_type=MESH).wait_send()
+
+    o_sent(0, tp)
+
+    @pl.when(mid == 1)
+    def _():
+        for k in (1, 2, 3):
+            o_sent(k, peer_shard(tp, k))
 
 
 def solution(mesh):
@@ -567,7 +572,7 @@
                 pltpu.VMEM((2, 4 * chunk, 2 * HEAD_DIM), BF16),
                 pltpu.VMEM((1, 4 * chunk), jnp.int32),
                 dma((n_blk + 6,)), dma((2, 3)), dma((2, 3)), dma((3,)), dma((3,)), dma((6,)), dma((6,)), dma((5,)), dma((4,)),
-                dma((4, 13)), dma((4, 13)), dma((5, n_pc)), dma((4, n_pc)),
+                dma((4,)), dma((4, 7)), dma((4,)), dma((4, n_pc)),
             ],
             compiler_params=pltpu.CompilerParams(collective_id=0, has_side_effects=True, vmem_limit_bytes=59600000),
         )(x_loc, seg_loc[None, :], w_query, w_key, w_value, w_out)

time: 166 us -> 164 us (0.988)
  no operation moved by 1% of the time
where the time goes in v7:
time: 164 us
  Pallas kernels  161 us (98%)
  local copies, waits for them, and re-layouts  3.05 us (2%)
    pallas_call x1, Pallas kernels, layer(): pl.pallas_call(layer_kernel, name='layer', out_shape=pltpu.VMEM((chunk, w...  161 us

profile of v7, /device:TPU:0, one launch (start us, length us, event | category | flops | bytes accessed | tf_op | source)
XLA Modules:
  0.0 163.8 jit_solution(749804259273725601)
XLA Ops:
  0.0 160.7 %layer.1 = bf16[1024,3584]{1,0:T(8,128)(2,1)S(1)} custom-call(bf16[1024,3584]{1,0:T(8,128)(2,1)} %x_hbm.1, s32[1,1024]{1,0:T(1,128)} %bitcast.1, bf16[3584,896]{1,0:T(8,128)(2,1)} %wq_hbm.1, bf16[3584,128]{1,0:T(8,128)(2,1)} %wk_hbm.1, bf16[3584,128]{1,0:T(8,128)(2,1)} %wv_hbm.1, bf16[896,3584]{1,0:T(8,128)(2,1)} %wo_hbm.1), custom_call_target="tpu_custom_call" | custom-call | tf_op jit(solution)/shard_map/layer/pallas_call | solution.py:563
  160.7 3.1 %copy.8 = bf16[1024,3584]{1,0:T(8,128)(2,1)} copy(bf16[1024,3584]{1,0:T(8,128)(2,1)S(1)} %layer.1) | data formatting | bytes 14680064

commit v8 on v7

--- a/solution.py
+++ b/solution.py
@@ -150,11 +150,24 @@
     def piece(c):
         return pl.ds(pl.multiple_of(c * O_ROWS, O_ROWS), O_ROWS)
 
+    def each(first, what):
+        @pl.loop(first, n_pc - per_blk)
+        def _(n):
+            what(nth(n))
+
+        for c in range(per_blk):
+            what(c)
+
     def nth(n):
         return (n_blk - 1 - n // per_blk) * per_blk + lax.rem(n, per_blk)
 
+    o_cut = q_cols - 2 * HEAD_DIM
+
     def o_copy(slot, c, shard, to):
-        at = o_v.at[shard, piece(c)]
+        if isinstance(c, int):
+            at = o_v.at[shard, 0:Q_BLK, slice(0, o_cut) if c == 0 else slice(o_cut, q_cols)]
+        else:
+            at = o_v.at[shard, piece(c)]
         return pltpu.make_async_remote_copy(at, at, o_send.at[slot], o_recv.at[shard, c], device_id=(dp, to, cp), device_id_type=MESH)
 
     def o_own(c):
@@ -162,7 +175,7 @@
 
     def o_leave(i):
         for j in range(per_blk):
-            o_own(i * per_blk + j).start()
+            o_own(j if isinstance(i, int) else i * per_blk + j).start()
 
     def o_next(k, c):
         shard = peer_shard(tp, k)
@@ -462,10 +475,11 @@
             w_relay(1, 1, 4)
             w_relay(2, 1, 4)
 
-            @pl.loop(0, n_pc)
-            def _(n):
-                o_forward(1, nth(n))
-                o_forward(2, nth(n))
+            def both(c):
+                o_forward(1, c)
+                o_forward(2, c)
+
+            each(0, both)
 
             w_relay(3, 0, 3, 1, 4)
             w_relay(1, 2, 5)
@@ -495,38 +509,45 @@
         multiply((0, 1), slice(None), n_tile, begin, during_first)
         w_finish(2)
 
-        @pl.loop(0, n_pc)
-        def _(n):
-            pl.when(mid == 0)(lambda: o_next(2, nth(n)).wait_recv())
-            pl.when((mid == 1) & (n < n_pc // 2))(lambda: o_forward(3, nth(n)))
+        pl.when(mid == 0)(lambda: each(0, lambda c: o_next(2, c).wait_recv()))
+
+        @pl.when(mid == 1)
+        def _():
+            @pl.loop(0, n_pc // 2)
+            def _(n):
+                o_forward(3, nth(n))
 
         multiply((2,), slice(None), n_tile, add, during_second)
         w_finish(3)
 
-        @pl.when(mid == 1)
-        def _():
-            @pl.loop(n_pc // 2, n_pc)
-            def _(n):
-                o_forward(3, nth(n))
-
-        def last_shard(first, pieces):
-            row0 = chunk - (first + pieces) * O_ROWS if pieces > 1 else (first - (n_pc - per_blk)) * O_ROWS
-            rows = pl.ds(row0, pieces * O_ROWS)
-
+        pl.when(mid == 1)(lambda: each(n_pc // 2, lambda c: o_forward(3, c)))
+
+        def last_shard(rows, pieces, cols, width, store):
             @pl.when(mid == 0)
             def _():
-                for n in range(first, first + pieces):
-                    o_next(3, nth(n)).wait_recv()
-
-            def store(out, part):
-                y_ref[rows, out] = (acc_v[rows, out] + part).astype(BF16)
-
-            multiply((3,), rows, 2 * n_tile, store, None)
-
-        last_shard(0, n_pc // 2)
-        last_shard(n_pc // 2, per_blk)
-        for n in range(n_pc - per_blk, n_pc):
-            last_shard(n, 1)
+                for c in pieces:
+                    o_next(3, c).wait_recv()
+
+            shard = peer_shard(tp, 3)
+
+            @pl.loop(0, n_cols // width)
+            def _(n):
+                out = pl.ds(pl.multiple_of(n * width, HEAD_DIM), width)
+                store(rows, out, jnp.dot(o_v[shard, rows, cols], w_v[shard, cols, out], preferred_element_type=F32))
+
+        def settle(rows, out, part):
+            y_ref[rows, out] = (acc_v[rows, out] + part).astype(BF16)
+
+        def gather(rows, out, part):
+            acc_v[rows, out] += part
+
+        def leaving(lo, hi):
+            return [jnp.int32((n_blk - 1 - n // per_blk) * per_blk + n % per_blk) for n in range(lo, hi)]
+
+        last_shard(slice(chunk // 2, chunk), leaving(0, n_pc // 2), slice(0, q_cols), 2 * n_tile, settle)
+        last_shard(slice(Q_BLK, chunk // 2), leaving(n_pc // 2, n_pc - per_blk), slice(0, q_cols), 2 * n_tile, settle)
+        last_shard(slice(0, Q_BLK), [0], slice(0, o_cut), n_cols // 4, gather)
+        last_shard(slice(0, Q_BLK), [1], slice(o_cut, q_cols), n_cols // 2, settle)
 
     pl.run_scoped(output, pltpu.VMEM((chunk, n_cols), F32))
 

time: 164 us -> 163 us (level)
  no operation moved by 1% of the time
where the time goes in v8:
time: 163 us
  Pallas kernels  160 us (98%)
  local copies, waits for them, and re-layouts  3.05 us (2%)
    pallas_call x1, Pallas kernels, layer(): pl.pallas_call(layer_kernel, name='layer', out_shape=pltpu.VMEM((chunk, w...  160 us

profile of v8, /device:TPU:0, one launch (start us, length us, event | category | flops | bytes accessed | tf_op | source)
XLA Modules:
  0.0 163.0 jit_solution(13913658184856586696)
XLA Ops:
  0.0 160.0 %layer.1 = bf16[1024,3584]{1,0:T(8,128)(2,1)S(1)} custom-call(bf16[1024,3584]{1,0:T(8,128)(2,1)} %x_hbm.1, s32[1,1024]{1,0:T(1,128)} %bitcast.1, bf16[3584,896]{1,0:T(8,128)(2,1)} %wq_hbm.1, bf16[3584,128]{1,0:T(8,128)(2,1)} %wk_hbm.1, bf16[3584,128]{1,0:T(8,128)(2,1)} %wv_hbm.1, bf16[896,3584]{1,0:T(8,128)(2,1)} %wo_hbm.1), custom_call_target="tpu_custom_call" | custom-call | tf_op jit(solution)/shard_map/layer/pallas_call | solution.py:584
  160.0 3.1 %copy.8 = bf16[1024,3584]{1,0:T(8,128)(2,1)} copy(bf16[1024,3584]{1,0:T(8,128)(2,1)S(1)} %layer.1) | data formatting | bytes 14680064
